TPU v7x, 16 devices: a whole 2x2x2 slice. The times are simulated.
16 devices in a mesh: dp: 16 (over z, y, x, core).
Axes of the slice: x: 2, y: 2, z: 2, core: 2. Of those that a mesh axis runs over, the one named last changes fastest.
Arguments:
- g_mat: bfloat16 [16, 25165824], P('dp')
- g_vec: bfloat16 [16, 26624], P('dp')
- p_mat: float32 [25165824], P('dp')
- m_mat: float32 [25165824], P('dp')
- v_mat: float32 [25165824], P('dp')
- p_vec: float32 [26624], replicated
- m_vec: float32 [26624], replicated
- v_vec: float32 [26624], replicated
- learn_rate: float32 [], replicated
Outputs:
- output 1: float32 [25165824], P('dp')
- output 2: float32 [25165824], P('dp')
- output 3: float32 [25165824], P('dp')
- output 4: float32 [26624], replicated
- output 5: float32 [26624], replicated
- output 6: float32 [26624], replicated
- output 7: bfloat16 [25165824], replicated
All inputs are finite; a program needn't handle non-finite values.
Results may differ from a plain program's by a relative error of at most 0.001.
Values are sent between devices in bfloat16 or wider.
A program may use at most 1 GiB of HBM per device.

v0:
```python
import jax
import jax.numpy as jnp
from jax import lax
from jax.sharding import PartitionSpec as P

STEP = 10
ADAM_BETA1 = 0.9
ADAM_BETA2 = 0.98
ADAM_EPS = 1e-8
WEIGHT_DECAY = 0.01
MAX_NORM = 1.0
NORM_EPS = 1e-6
BIAS_ONE = 1.0 - ADAM_BETA1 ** STEP
BIAS_TWO = 1.0 - ADAM_BETA2 ** STEP


def adam_update(grad_vals, param_vals, moment_one, moment_two, learn_rate, decay_rate):
    new_one = ADAM_BETA1 * moment_one + (1.0 - ADAM_BETA1) * grad_vals
    new_two = ADAM_BETA2 * moment_two + (1.0 - ADAM_BETA2) * grad_vals * grad_vals
    direction = (new_one / BIAS_ONE) / (jnp.sqrt(new_two / BIAS_TWO) + ADAM_EPS)
    return param_vals - learn_rate * (direction + decay_rate * param_vals), new_one, new_two


def solution(mesh):
    axis_name = mesh.axis_names[0]
    group_size = mesh.shape[axis_name]

    def local_step(g_mat, g_vec, p_mat, m_mat, v_mat, p_vec, m_vec, v_vec, learn_rate):
        send_rows = g_mat.reshape(group_size, -1)
        recv_rows = lax.all_to_all(send_rows, axis_name, 0, 0, tiled=True)
        grad_mat = jnp.sum(recv_rows.astype(jnp.float32), axis=0) / group_size
        grad_vec = lax.psum(g_vec[0].astype(jnp.float32), axis_name) / group_size
        norm_sq = lax.psum(jnp.sum(grad_mat * grad_mat), axis_name) + jnp.sum(grad_vec * grad_vec)
        clip_scale = jnp.minimum(1.0, MAX_NORM / (jnp.sqrt(norm_sq) + NORM_EPS))
        new_p_mat, new_m_mat, new_v_mat = adam_update(grad_mat * clip_scale, p_mat, m_mat, v_mat, learn_rate, WEIGHT_DECAY)
        new_p_vec, new_m_vec, new_v_vec = adam_update(grad_vec * clip_scale, p_vec, m_vec, v_vec, learn_rate, 0.0)
        full_params = lax.all_gather(new_p_mat.astype(jnp.bfloat16), axis_name, tiled=True)
        return new_p_mat, new_m_mat, new_v_mat, new_p_vec, new_m_vec, new_v_vec, full_params

    return jax.shard_map(
        local_step,
        mesh=mesh,
        in_specs=(P(axis_name, None), P(axis_name, None), P(axis_name), P(axis_name), P(axis_name), P(), P(), P(), P()),
        out_specs=(P(axis_name), P(axis_name), P(axis_name), P(), P(), P(), P()),
        check_vma=False,
    )
```

profile of v0, /device:TPU:0, one launch (start us, length us, event | category | flops | bytes accessed | tf_op | source)
XLA Modules:
  0.0 1726.8 jit_solution(3099028963842223312)
XLA Ops:
  7.2 0.5 broadcast.8
  7.7 316.8 %reduce.1 = bf16[16,1572864]{1,0:T(8,128)(2,1)} reduce(bf16[16,1,1572864]{2,1,0:T(2,128)(2,1)} %bitcast, bf16[]{:T(256)} %broadcast.8), dimensions={1}, to_apply=%bitcast.reduce_sub_computation | reduce | bytes 100663296 | tf_op jit(solution)/shard_map/all_to_all | solution.py:30
  324.5 295.1 %reshape.22 = bf16[16,2,786432]{2,1,0:T(2,128)(2,1)} reshape(bf16[16,1572864]{1,0:T(8,128)(2,1)} %reduce.1) | data formatting | bytes 100663296
  619.6 0.0 copy-start.1
  619.6 5.5 all-to-all-start
  625.1 0.0 all-reduce.2.cloned.1.call-start
  625.2 0.0 copy-done.1
  625.2 0.8 convert_element_type.17
  625.9 0.0 all-reduce.2.cloned.1.call-update
  625.9 0.0 all-gather.2.cloned.1.call-start
  626.6 599.5 %all-to-all-done = bf16[16,2,786432]{2,1,0:T(2,128)(2,1)} async-done(((bf16[16,2,786432]{2,1,0:T(2,128)(2,1)}), bf16[16,2,786432]{2,1,0:T(2,128)(2,1)}, u32[]{:S(2)}, u32[]{:S(2)}) %all-to-all-start) | async-done | bytes 50331680 | tf_op jit(solution)/shard_map/all_to_all | solution.py:30
  1226.1 114.4 %reshape.23 = bf16[16,1,1572864]{2,1,0:T(2,128)(2,1)} reshape(bf16[16,2,786432]{2,1,0:T(2,128)(2,1)} %all-to-all-done) | data formatting | bytes 100663296
  1340.5 100.2 %convert_reduce_fusion = f32[1572864]{0:T(1024)} fusion(bf16[16,1,1572864]{2,1,0:T(2,128)(2,1)} %reshape.23), kind=kLoop, calls=%fused_computation | loop fusion | flops 48758784 | bytes 56623104 | tf_op jit(solution)/shard_map/reduce_sum | solution.py:31
  1440.8 4.3 multiply_reduce_fusion
  1445.0 0.0 all-reduce.2.cloned.1.call-done
  1445.0 1.5 multiply_reduce_fusion.1
  1446.6 33.1 %psum.14 = f32[]{:T(128)} all-reduce(f32[]{:T(128)} %multiply_reduce_fusion), channel_id=1, replica_groups=mesh['dp'=16] {'dp'}, use_global_device_ids=true, to_apply=%region_2.0 | all-reduce | flops 1 | bytes 8 | tf_op jit(solution)/shard_map/psum | solution.py:33
  1481.1 0.0 copy-start
  1481.1 0.0 copy-start.2
  1481.1 0.0 copy-start.3
  1481.1 0.0 copy-start.4
  1481.1 18.0 %fusion.2 = (bf16[1572864]{0:T(1024)(128)(2,1)}, f32[1572864]{0:T(1024)}, f32[1572864]{0:T(1024)}, f32[1572864]{0:T(1024)}) fusion(f32[1572864]{0:T(1024)} %param.11, f32[]{:T(128)S(6)} %copy.18, f32[1572864]{0:T(1024)} %convert_reduce_fusion, f32[]{:T(128)S(6)} %mul.103, f32[1572864]{0:T(1024)} %param.12, f32[1572864]{0:T(1024)} %param.13), kind=kLoop, calls=%fused_computation.11 | loop fusion | flops 26738688 | bytes 47185928 | tf_op jit(solution)/shard_map/convert_element_type | solution.py:37
  1499.1 0.0 all-gather.2.cloned.1.call-update
  1499.2 0.0 copy-done
  1499.2 0.0 copy-done.2
  1499.2 0.0 copy-done.3
  1499.2 0.0 copy-done.4
  1499.2 0.8 multiply_subtract_fusion.1
  1500.0 186.3 %all-gather.2.cloned.1.call-done = bf16[25165824]{0:T(1024)(128)(2,1)} async-done(((bf16[1572864]{0:T(1024)(128)(2,1)}), bf16[25165824]{0:T(1024)(128)(2,1)}) %all-gather.2.cloned.1.call-update) | async-done | bytes 50331664 | tf_op jit(solution)/shard_map/all_gather | solution.py:37
  1686.3 33.4 %copy.19 = bf16[25165824]{0:T(1024)(128)(2,1)} copy(bf16[25165824]{0:T(1024)(128)(2,1)} %all-gather.2.cloned.1.call-done) | data formatting | bytes 100663296
Async XLA Ops:
  619.6 5.5 copy-start.1
  619.6 606.4 %all-to-all-start = ((bf16[16,2,786432]{2,1,0:T(2,128)(2,1)}), bf16[16,2,786432]{2,1,0:T(2,128)(2,1)}, u32[]{:S(2)}, u32[]{:S(2)}) async-start(bf16[16,2,786432]{2,1,0:T(2,128)(2,1)} %reshape.22), calls=%async_computation | async-start | bytes 100663296 | tf_op jit(solution)/shard_map/all_to_all | solution.py:30
  625.1 819.9 %all-reduce.2.cloned.1.call-start = ((), (), s32[]{:S(2)}) async-start(), calls=%async_computation.1 | async-start | bytes 212992 | tf_op jit(solution)/shard_map/psum | solution.py:32
  625.9 1060.3 %all-gather.2.cloned.1.call-start = ((), (), s32[]{:S(2)}) async-start(), calls=%async_computation.2 | async-start | bytes 53477376 | tf_op jit(solution)/shard_map/all_gather | solution.py:37
  1481.1 18.1 %copy-start = (f32[26624]{0:T(1024)S(1)}, f32[26624]{0:T(1024)}, u32[]{:S(2)}) copy-start(f32[26624]{0:T(1024)} %all-reduce.2.cloned.1.call-done) | copy-start | bytes 319492
  1481.1 18.1 %copy-start.2 = (f32[26624]{0:T(1024)S(1)}, f32[26624]{0:T(1024)}, u32[]{:S(2)}) copy-start(f32[26624]{0:T(1024)} %param.14) | copy-start | bytes 319492
  1481.1 18.1 %copy-start.3 = (f32[26624]{0:T(1024)S(1)}, f32[26624]{0:T(1024)}, u32[]{:S(2)}) copy-start(f32[26624]{0:T(1024)} %param.15) | copy-start | bytes 319492
  1481.1 18.1 %copy-start.4 = (f32[26624]{0:T(1024)S(1)}, f32[26624]{0:T(1024)}, u32[]{:S(2)}) copy-start(f32[26624]{0:T(1024)} %param.16) | copy-start | bytes 319492
Sparse Core Ops, SparseCore 0:
  630.7 505.9 all-reduce.1
  1499.3 186.9 all-gather.1
where the time goes:
time: 1730 us
  waiting for transfers between devices  786 us (45%)
  local copies, waits for them, and re-layouts  444 us (26%)
  other arithmetic  442 us (26%)
  blocking collectives  33.1 us (2%)
    all_to_all x1, waiting for transfers between devices, local_step(): recv_rows = lax.all_to_all(send_rows, axis_name, 0, 0, tiled=True)  599 us
    unnamed x13, local copies, waits for them, and re-layouts  443 us
    all_to_all x1, other arithmetic, local_step(): recv_rows = lax.all_to_all(send_rows, axis_name, 0, 0, tiled=True)  317 us
    all_gather x1, waiting for transfers between devices, local_step(): lax.all_gather(new_p_mat.astype(jnp.bfloat16), axis_name, tiled=True)  186 us
    reduce_sum x1, other arithmetic, local_step(): grad_mat = jnp.sum(recv_rows.astype(jnp.float32), axis=0) / group_size  100 us
  transfers between devices with their start and end apart: 3, of which 2 were waited for; matrix products, arithmetic and copies ran while one was open for 13% of the time, Pallas kernels for 0%

commit v1 on v0

--- a/solution.py
+++ b/solution.py
@@ -1,6 +1,10 @@
+import functools
+
 import jax
 import jax.numpy as jnp
 from jax import lax
+from jax.experimental import pallas as pl
+from jax.experimental.pallas import tpu as pltpu
 from jax.sharding import PartitionSpec as P
 
 STEP = 10
@@ -13,6 +17,12 @@
 BIAS_ONE = 1.0 - ADAM_BETA1 ** STEP
 BIAS_TWO = 1.0 - ADAM_BETA2 ** STEP
 
+MESH_ID = pl.DeviceIdType.MESH
+COLORS = 3
+PARTS = 4
+STRIDES = (2, 4, 8)
+STEPS = 8 * PARTS
+
 
 def adam_update(grad_vals, param_vals, moment_one, moment_two, learn_rate, decay_rate):
     new_one = ADAM_BETA1 * moment_one + (1.0 - ADAM_BETA1) * grad_vals
@@ -21,14 +31,215 @@
     return param_vals - learn_rate * (direction + decay_rate * param_vals), new_one, new_two
 
 
+def scatter_kernel(axis_name, piece, g, out, pg, a_buf, b_buf, stage, r1, r2, r3,
+                   a_sem, b_sem, ds_sem, dr_sem, s1_sem, r1_sem, s2_sem, r2_sem, s3_sem, r3_sem, o_sem):
+    chunk = piece // (COLORS * PARTS)
+    me = lax.axis_index(axis_name)
+    core_step = 1 - 2 * lax.rem(me, 2)
+    deltas = [s * (1 - 2 * lax.rem(me // s, 2)) for s in STRIDES]
+    partner = me + core_step
+    peers = [me + d for d in deltas]
+
+    barrier = pltpu.get_barrier_semaphore()
+    for dev in (partner, *peers):
+        pl.semaphore_signal(barrier, inc=1, device_id=(dev,), device_id_type=MESH_ID)
+
+    def offset(color, t):
+        unit = t // PARTS
+        f1 = 1 - unit // 4
+        f2 = 1 - lax.rem(unit // 2, 2)
+        f3 = 1 - lax.rem(unit, 2)
+        d1, d2, d3 = (deltas[(color + k) % 3] for k in range(3))
+        owner = me + f1 * d1 + f2 * d2 + f3 * d3
+        return owner * piece + (color * PARTS + lax.rem(t, PARTS)) * chunk
+
+    def cut(ref, start):
+        return ref.at[:, pl.ds(pl.multiple_of(start, 1024), chunk)]
+
+    def swap(color, t):
+        return pltpu.make_async_remote_copy(
+            src_ref=cut(g, offset(color, t) + core_step * piece),
+            dst_ref=cut(pg, (color * STEPS + t) * chunk),
+            send_sem=ds_sem.at[color * 4 + lax.rem(t, 4)],
+            recv_sem=dr_sem.at[color * STEPS + t],
+            device_id=(partner,), device_id_type=MESH_ID)
+
+    def load_a(color, t):
+        k = color * 2 + lax.rem(t, 2)
+        return pltpu.make_async_copy(cut(g, offset(color, t)), a_buf.at[k], a_sem.at[k])
+
+    def load_b(color, t):
+        k = color * 2 + lax.rem(t, 2)
+        return pltpu.make_async_copy(cut(pg, (color * STEPS + t) * chunk), b_buf.at[k], b_sem.at[k])
+
+    def push(src, dst, send_sem, recv_sem, axis):
+        return pltpu.make_async_remote_copy(
+            src_ref=src, dst_ref=dst, send_sem=send_sem, recv_sem=recv_sem,
+            device_id=(peers[axis],), device_id_type=MESH_ID)
+
+    def push1(color, t):
+        k = color * 3 + lax.rem(t, 3)
+        j = color * 4 * PARTS + t
+        return push(stage.at[k], r1.at[j], s1_sem.at[k], r1_sem.at[j], color)
+
+    def push2(color, t):
+        j = color * 2 * PARTS + t - 4 * PARTS
+        return push(r1.at[color * 4 * PARTS + t - 4 * PARTS], r2.at[j], s2_sem.at[j], r2_sem.at[j], (color + 1) % 3)
+
+    def push3(color, t):
+        j = color * PARTS + t - 6 * PARTS
+        return push(r1.at[color * 4 * PARTS + t - 4 * PARTS], r3.at[j], s3_sem.at[j], r3_sem.at[j], (color + 2) % 3)
+
+    def store(color, t):
+        j = color * PARTS + t - 7 * PARTS
+        return pltpu.make_async_copy(r3.at[j], cut(out, j * chunk), o_sem.at[j])
+
+    def add_up(color, t, dst, extra):
+        k = color * 2 + lax.rem(t, 2)
+        width = min(chunk, 4096)
+
+        @pl.loop(0, chunk // width)
+        def _(i):
+            s = pl.ds(pl.multiple_of(i * width, width), width)
+            acc = a_buf[k, :, s].astype(jnp.float32) + b_buf[k, :, s].astype(jnp.float32)
+            for ref, j in extra:
+                acc = acc + ref[j, :, s]
+            dst[0][dst[1], :, s] = acc
+
+    def ready(color, t):
+        load_a(color, t).wait()
+        load_b(color, t).wait()
+
+    def refill(color, t):
+        load_a(color, t).start()
+        swap(color, t).wait_recv()
+        load_b(color, t).start()
+
+    def more_swap(color, t):
+        swap(color, t - 4).wait_send()
+        swap(color, t).start()
+
+    for t in range(2):
+        for color in range(COLORS):
+            load_a(color, t).start()
+    pl.semaphore_wait(barrier, 4)
+    for t in range(4):
+        for color in range(COLORS):
+            swap(color, t).start()
+    for t in range(2):
+        for color in range(COLORS):
+            swap(color, t).wait_recv()
+            load_b(color, t).start()
+
+    def phase_one(t, first):
+        for color in range(COLORS):
+            ready(color, t)
+            if not first:
+                push1(color, t - 3).wait_send()
+            add_up(color, t, (stage, color * 3 + lax.rem(t, 3)), ())
+            push1(color, t).start()
+            more_swap(color, t + 4)
+            refill(color, t + 2)
+
+    def run(lo, hi, body):
+        lax.fori_loop(lo, hi, lambda t, c: (body(t), c)[1], 0)
+
+    run(0, 3, lambda t: phase_one(t, True))
+    run(3, 4 * PARTS, lambda t: phase_one(t, False))
+
+    def phase_two(t):
+        for color in range(COLORS):
+            ready(color, t)
+            j = color * 4 * PARTS + t - 4 * PARTS
+            push1(color, t - 4 * PARTS).wait_recv()
+            add_up(color, t, (r1, j), ((r1, j),))
+            push2(color, t).start()
+            more_swap(color, t + 4)
+            refill(color, t + 2)
+
+    run(4 * PARTS, 6 * PARTS, phase_two)
+
+    def phase_three(t):
+        for color in range(COLORS):
+            ready(color, t)
+            j = color * 4 * PARTS + t - 4 * PARTS
+            push1(color, t - 4 * PARTS).wait_recv()
+            push2(color, t - 2 * PARTS).wait_recv()
+            add_up(color, t, (r1, j), ((r1, j), (r2, color * 2 * PARTS + t - 6 * PARTS)))
+            push3(color, t).start()
+            more_swap(color, t + 4)
+            refill(color, t + 2)
+
+    run(6 * PARTS, 7 * PARTS, phase_three)
+
+    def phase_four(t, fill):
+        for color in range(COLORS):
+            ready(color, t)
+            push1(color, t - 4 * PARTS).wait_recv()
+            push2(color, t - 2 * PARTS).wait_recv()
+            push3(color, t - PARTS).wait_recv()
+            add_up(color, t, (r3, color * PARTS + t - 7 * PARTS), (
+                (r1, color * 4 * PARTS + t - 4 * PARTS),
+                (r2, color * 2 * PARTS + t - 6 * PARTS),
+                (r3, color * PARTS + t - 7 * PARTS)))
+            store(color, t).start()
+            if fill:
+                refill(color, t + 2)
+
+    run(7 * PARTS, 7 * PARTS + 2, lambda t: phase_four(t, True))
+    run(7 * PARTS + 2, STEPS, lambda t: phase_four(t, False))
+
+    def drain(lo, hi, wait):
+        def body(t):
+            for color in range(COLORS):
+                wait(color, t)
+        run(lo, hi, body)
+
+    drain(4 * PARTS - 3, 4 * PARTS, lambda c, t: push1(c, t).wait_send())
+    drain(4 * PARTS, 6 * PARTS, lambda c, t: push2(c, t).wait_send())
+    drain(6 * PARTS, 7 * PARTS, lambda c, t: push3(c, t).wait_send())
+    drain(STEPS - 4, STEPS, lambda c, t: swap(c, t).wait_send())
+    drain(7 * PARTS, STEPS, lambda c, t: store(c, t).wait())
+
+
+def scatter_sum(g_mat, axis_name, group_size):
+    total = g_mat.shape[1]
+    piece = total // group_size
+    chunk = piece // (COLORS * PARTS)
+    dma = pltpu.SemaphoreType.DMA
+    out, _ = pl.pallas_call(
+        functools.partial(scatter_kernel, axis_name, piece),
+        out_shape=(jax.ShapeDtypeStruct((1, piece), jnp.float32),
+                   jax.ShapeDtypeStruct((1, total // 2), jnp.bfloat16)),
+        in_specs=[pl.BlockSpec(memory_space=pl.ANY)],
+        out_specs=[pl.BlockSpec(memory_space=pl.ANY)] * 2,
+        scratch_shapes=[
+            pltpu.VMEM((2 * COLORS, 1, chunk), jnp.bfloat16),
+            pltpu.VMEM((2 * COLORS, 1, chunk), jnp.bfloat16),
+            pltpu.VMEM((3 * COLORS, 1, chunk), jnp.float32),
+            pltpu.VMEM((4 * PARTS * COLORS, 1, chunk), jnp.float32),
+            pltpu.VMEM((2 * PARTS * COLORS, 1, chunk), jnp.float32),
+            pltpu.VMEM((PARTS * COLORS, 1, chunk), jnp.float32),
+            dma((2 * COLORS,)), dma((2 * COLORS,)),
+            dma((4 * COLORS,)), dma((STEPS * COLORS,)),
+            dma((3 * COLORS,)), dma((4 * PARTS * COLORS,)),
+            dma((2 * PARTS * COLORS,)), dma((2 * PARTS * COLORS,)),
+            dma((PARTS * COLORS,)), dma((PARTS * COLORS,)),
+            dma((PARTS * COLORS,)),
+        ],
+        compiler_params=pltpu.CompilerParams(
+            collective_id=0, has_side_effects=True, vmem_limit_bytes=63 * 1024 * 1024),
+        name="scatter_sum",
+    )(g_mat)
+    return out.reshape(piece)
+
+
 def solution(mesh):
     axis_name = mesh.axis_names[0]
     group_size = mesh.shape[axis_name]
 
     def local_step(g_mat, g_vec, p_mat, m_mat, v_mat, p_vec, m_vec, v_vec, learn_rate):
-        send_rows = g_mat.reshape(group_size, -1)
-        recv_rows = lax.all_to_all(send_rows, axis_name, 0, 0, tiled=True)
-        grad_mat = jnp.sum(recv_rows.astype(jnp.float32), axis=0) / group_size
+        grad_mat = scatter_sum(g_mat, axis_name, group_size) / group_size
         grad_vec = lax.psum(g_vec[0].astype(jnp.float32), axis_name) / group_size
         norm_sq = lax.psum(jnp.sum(grad_mat * grad_mat), axis_name) + jnp.sum(grad_vec * grad_vec)
         clip_scale = jnp.minimum(1.0, MAX_NORM / (jnp.sqrt(norm_sq) + NORM_EPS))

time: 1730 us -> 640 us (0.37)
  waiting for transfers between devices: 786 us -> 186 us
  local copies, waits for them, and re-layouts: 444 us -> 33.5 us
  other arithmetic: 442 us -> 37.7 us
  Pallas kernels: 0 us -> 334 us
    all_to_all x1 -> x0, waiting for transfers between devices: 599 us -> none  [local_step(): recv_rows = lax.all_to_all(send_rows, axis_name, 0, 0, tiled=True)]
    unnamed x13 -> x9, local copies, waits for them, and re-layouts: 443 us -> 33.5 us
    pallas_call x0 -> x1, Pallas kernels: none -> 334 us  [scatter_sum(): pl.pallas_call(functools.partial(scatter_kernel, axis_name, piece), out_s...]
    all_to_all x1 -> x0, other arithmetic: 317 us -> none  [local_step(): recv_rows = lax.all_to_all(send_rows, axis_name, 0, 0, tiled=True)]
    reduce_sum x1 -> x0, other arithmetic: 100 us -> none  [local_step(): grad_mat = jnp.sum(recv_rows.astype(jnp.float32), axis=0) / group_size]
  transfers between devices with their start and end apart: 3 -> 2, of which waited for: 2 -> 1; matrix products, arithmetic and copies ran while one was open for 13% -> 2% of each run, Pallas kernels for 0% -> 52%
where the time goes in v1:
time: 640 us; the launch traced here: 639 us
  Pallas kernels  334 us (52%)
  waiting for transfers between devices  186 us (29%)
  other arithmetic  37.7 us (6%)
  local copies, waits for them, and re-layouts  33.5 us (5%)
  blocking collectives  31.9 us (5%)
  between operations  16.2 us (3%)
    pallas_call x1, Pallas kernels, scatter_sum(): pl.pallas_call(functools.partial(scatter_kernel, axis_name, piece), out_s...  334 us
    all_gather x1, waiting for transfers between devices, local_step(): lax.all_gather(new_p_mat.astype(jnp.bfloat16), axis_name, tiled=True)  186 us
    unnamed x9, local copies, waits for them, and re-layouts  33.5 us
    psum x1, blocking collectives, local_step(): lax.psum(jnp.sum(grad_mat * grad_mat), axis_name)  31.9 us
    reduce_sum x1, other arithmetic, local_step(): jnp.sum(grad_mat * grad_mat)  14.6 us
    convert_element_type x1, other arithmetic, local_step(): new_p_mat.astype(jnp.bfloat16)  13.6 us
  transfers between devices with their start and end apart: 2, of which 1 were waited for; matrix products, arithmetic and copies ran while one was open for 2% of the time, Pallas kernels for 52%

profile of v1, /device:TPU:0, one launch (start us, length us, event | category | flops | bytes accessed | tf_op | source)
XLA Modules:
  0.0 639.3 jit_solution(10763961753143127978)
XLA Ops:
  7.2 0.0 all-reduce.2.cloned.1.call-start
  7.2 1.6 convert_element_type.12
  8.9 0.0 all-reduce.2.cloned.1.call-update
  8.9 0.0 all-gather.2.cloned.1.call-start
  8.9 333.6 %scatter_sum.1 = (f32[1,1572864]{1,0:T(1,128)}, bf16[1,12582912]{1,0:T(2,128)(2,1)}) custom-call(bf16[1,25165824]{1,0:T(2,128)(2,1)} %g.1), custom_call_target="tpu_custom_call" | custom-call | tf_op jit(solution)/shard_map/scatter_sum/pallas_call | solution.py:210
  342.5 14.6 %multiply_reduce_fusion = f32[]{:T(128)} fusion(f32[1,1572864]{1,0:T(1,128)} %get-tuple-element.8), kind=kLoop, calls=%fused_computation.4 | loop fusion | flops 4718591 | bytes 6291460 | tf_op jit(solution)/shard_map/reduce_sum | solution.py:244
  357.2 31.9 %psum.14 = f32[]{:T(128)} all-reduce(f32[]{:T(128)} %multiply_reduce_fusion), channel_id=1, replica_groups=mesh['dp'=16] {'dp'}, use_global_device_ids=true, to_apply=%region_1.0 | all-reduce | flops 1 | bytes 8 | tf_op jit(solution)/shard_map/psum | solution.py:244
  389.7 0.0 all-reduce.2.cloned.1.call-done
  389.8 1.5 multiply_reduce_fusion.1
  392.7 5.6 broadcast_multiply_fusion
  398.2 0.0 copy-start
  398.2 0.0 copy-start.1
  398.3 0.0 copy-start.2
  398.3 0.0 copy-start.3
  398.3 13.6 %fusion.2 = (bf16[1572864]{0:T(1024)(128)(2,1)}, f32[1572864]{0:T(1024)}, f32[1572864]{0:T(1024)}, f32[1572864]{0:T(1024)}) fusion(f32[1572864]{0:T(1024)} %param.11, f32[]{:T(128)S(6)} %copy.18, f32[1572864]{0:T(1024)S(1)} %bitcast.2, f32[1572864]{0:T(1024)} %param.12, f32[1572864]{0:T(1024)} %param.13), kind=kLoop, calls=%fused_computation.11 | loop fusion | flops 25165824 | bytes 47185924 | tf_op jit(solution)/shard_map/convert_element_type | solution.py:248
  411.9 0.0 all-gather.2.cloned.1.call-update
  411.9 0.0 copy-done
  411.9 0.0 copy-done.1
  411.9 0.0 copy-done.2
  411.9 0.0 copy-done.3
  411.9 0.8 multiply_subtract_fusion.1
  412.7 186.3 %all-gather.2.cloned.1.call-done = bf16[25165824]{0:T(1024)(128)(2,1)} async-done(((bf16[1572864]{0:T(1024)(128)(2,1)}), bf16[25165824]{0:T(1024)(128)(2,1)}) %all-gather.2.cloned.1.call-update) | async-done | bytes 50331664 | tf_op jit(solution)/shard_map/all_gather | solution.py:248
  599.0 33.4 %copy.19 = bf16[25165824]{0:T(1024)(128)(2,1)} copy(bf16[25165824]{0:T(1024)(128)(2,1)} %all-gather.2.cloned.1.call-done) | data formatting | bytes 100663296
Async XLA Ops:
  7.2 382.6 %all-reduce.2.cloned.1.call-start = ((), (), s32[]{:S(2)}) async-start(), calls=%async_computation | async-start | bytes 212992 | tf_op jit(solution)/shard_map/psum | solution.py:243
  8.9 590.1 %all-gather.2.cloned.1.call-start = ((), (), s32[]{:S(2)}) async-start(), calls=%async_computation.1 | async-start | bytes 53477376 | tf_op jit(solution)/shard_map/all_gather | solution.py:248
  398.2 13.6 %copy-start = (f32[26624]{0:T(1024)S(1)}, f32[26624]{0:T(1024)}, u32[]{:S(2)}) copy-start(f32[26624]{0:T(1024)} %all-reduce.2.cloned.1.call-done) | copy-start | bytes 319492
  398.2 13.6 %copy-start.1 = (f32[26624]{0:T(1024)S(1)}, f32[26624]{0:T(1024)}, u32[]{:S(2)}) copy-start(f32[26624]{0:T(1024)} %param.14) | copy-start | bytes 319492
  398.3 13.6 %copy-start.2 = (f32[26624]{0:T(1024)S(1)}, f32[26624]{0:T(1024)}, u32[]{:S(2)}) copy-start(f32[26624]{0:T(1024)} %param.15) | copy-start | bytes 319492
  398.3 13.6 %copy-start.3 = (f32[26624]{0:T(1024)S(1)}, f32[26624]{0:T(1024)}, u32[]{:S(2)}) copy-start(f32[26624]{0:T(1024)} %param.16) | copy-start | bytes 319492
Sparse Core Ops, SparseCore 0:
  12.8 68.2 all-reduce.1
  412.0 186.9 all-gather.1

commit v2 on v1

--- a/solution.py
+++ b/solution.py
@@ -22,6 +22,9 @@
 PARTS = 4
 STRIDES = (2, 4, 8)
 STEPS = 8 * PARTS
+WIDTH = 4096
+WRITES = 16
+MEAN_SCALE = 1.0 / 16.0
 
 
 def adam_update(grad_vals, param_vals, moment_one, moment_two, learn_rate, decay_rate):
@@ -31,9 +34,13 @@
     return param_vals - learn_rate * (direction + decay_rate * param_vals), new_one, new_two
 
 
-def scatter_kernel(axis_name, piece, g, out, pg, a_buf, b_buf, stage, r1, r2, r3,
-                   a_sem, b_sem, ds_sem, dr_sem, s1_sem, r1_sem, s2_sem, r2_sem, s3_sem, r3_sem, o_sem):
+def scatter_kernel(axis_name, piece, g, gv, out, pg, vec_out, clip_out,
+                   a_buf, b_buf, stage, r1, r2, r3, v_in, v_acc, v_get, n_acc, n_get, squares,
+                   a_sem, b_sem, ds_sem, dr_sem, s1_sem, r1_sem, s2_sem, r2_sem, s3_sem, r3_sem, o_sem,
+                   vi_sem, vs_sem, vr_sem, ns_sem, nr_sem, vo_sem):
     chunk = piece // (COLORS * PARTS)
+    width = min(chunk, WIDTH)
+    n_vec = gv.shape[1]
     me = lax.axis_index(axis_name)
     core_step = 1 - 2 * lax.rem(me, 2)
     deltas = [s * (1 - 2 * lax.rem(me // s, 2)) for s in STRIDES]
@@ -94,9 +101,8 @@
         j = color * PARTS + t - 7 * PARTS
         return pltpu.make_async_copy(r3.at[j], cut(out, j * chunk), o_sem.at[j])
 
-    def add_up(color, t, dst, extra):
+    def add_up(color, t, dst, extra, last=False):
         k = color * 2 + lax.rem(t, 2)
-        width = min(chunk, 4096)
 
         @pl.loop(0, chunk // width)
         def _(i):
@@ -104,7 +110,33 @@
             acc = a_buf[k, :, s].astype(jnp.float32) + b_buf[k, :, s].astype(jnp.float32)
             for ref, j in extra:
                 acc = acc + ref[j, :, s]
+            if last:
+                acc = acc * MEAN_SCALE
+                squares[...] += acc * acc
             dst[0][dst[1], :, s] = acc
+
+    def vec_push(k):
+        return pltpu.make_async_remote_copy(
+            src_ref=v_acc.at[k], dst_ref=v_get.at[k], send_sem=vs_sem.at[k], recv_sem=vr_sem.at[k],
+            device_id=((partner, *peers)[k],), device_id_type=MESH_ID)
+
+    def norm_push(k):
+        return pltpu.make_async_remote_copy(
+            src_ref=n_acc.at[k], dst_ref=n_get.at[k], send_sem=ns_sem.at[k], recv_sem=nr_sem.at[k],
+            device_id=((partner, *peers)[k],), device_id_type=MESH_ID)
+
+    def vec_loop(body):
+        @pl.loop(0, n_vec // 1024)
+        def _(i):
+            body(pl.ds(pl.multiple_of(i * 1024, 1024), 1024))
+
+    def vec_turn(k):
+        def body(s):
+            v_acc[k + 1, :, s] = v_acc[k, :, s] + v_get[k, :, s]
+        vec_push(k).wait_recv()
+        vec_loop(body)
+        if k < 3:
+            vec_push(k + 1).start()
 
     def ready(color, t):
         load_a(color, t).wait()
@@ -122,6 +154,9 @@
     for t in range(2):
         for color in range(COLORS):
             load_a(color, t).start()
+    vec_load = pltpu.make_async_copy(gv, v_in, vi_sem)
+    vec_load.start()
+    squares[...] = jnp.zeros_like(squares)
     pl.semaphore_wait(barrier, 4)
     for t in range(4):
         for color in range(COLORS):
@@ -145,7 +180,27 @@
         lax.fori_loop(lo, hi, lambda t, c: (body(t), c)[1], 0)
 
     run(0, 3, lambda t: phase_one(t, True))
-    run(3, 4 * PARTS, lambda t: phase_one(t, False))
+    vec_load.wait()
+
+    def widen(s):
+        v_acc[0, :, s] = v_in[:, s].astype(jnp.float32)
+
+    vec_loop(widen)
+    vec_push(0).start()
+    for k in range(4):
+        run(3 * k + 3, 3 * k + 6, lambda t: phase_one(t, False))
+        vec_turn(k)
+    run(15, 4 * PARTS, lambda t: phase_one(t, False))
+
+    def vec_mean(s):
+        mean = v_acc[4, :, s] * MEAN_SCALE
+        v_acc[0, :, s] = mean
+        v_get[0, :, s] = mean * mean
+
+    vec_push(0).wait_send()
+    vec_loop(vec_mean)
+    vec_store = pltpu.make_async_copy(v_acc.at[0], vec_out, vo_sem)
+    vec_store.start()
 
     def phase_two(t):
         for color in range(COLORS):
@@ -181,13 +236,21 @@
             add_up(color, t, (r3, color * PARTS + t - 7 * PARTS), (
                 (r1, color * 4 * PARTS + t - 4 * PARTS),
                 (r2, color * 2 * PARTS + t - 6 * PARTS),
-                (r3, color * PARTS + t - 7 * PARTS)))
+                (r3, color * PARTS + t - 7 * PARTS)), last=True)
             store(color, t).start()
             if fill:
                 refill(color, t + 2)
 
     run(7 * PARTS, 7 * PARTS + 2, lambda t: phase_four(t, True))
     run(7 * PARTS + 2, STEPS, lambda t: phase_four(t, False))
+
+    n_acc[0] = jnp.broadcast_to(jnp.sum(squares[...], axis=1, keepdims=True), (1, 128))
+    for k in range(4):
+        norm_push(k).start()
+        norm_push(k).wait_recv()
+        n_acc[k + 1] = n_acc[k] + n_get[k]
+    norm_sq = n_acc[4] + jnp.sum(v_get[0], axis=1, keepdims=True)
+    clip_out[...] = jnp.minimum(1.0, MAX_NORM / (jnp.sqrt(norm_sq) + NORM_EPS))
 
     def drain(lo, hi, wait):
         def body(t):
@@ -200,19 +263,28 @@
     drain(6 * PARTS, 7 * PARTS, lambda c, t: push3(c, t).wait_send())
     drain(STEPS - 4, STEPS, lambda c, t: swap(c, t).wait_send())
     drain(7 * PARTS, STEPS, lambda c, t: store(c, t).wait())
-
-
-def scatter_sum(g_mat, axis_name, group_size):
+    for k in range(4):
+        norm_push(k).wait_send()
+        if k:
+            vec_push(k).wait_send()
+    vec_store.wait()
+
+
+def scatter_sum(g_mat, g_vec, axis_name, group_size):
     total = g_mat.shape[1]
+    n_vec = g_vec.shape[1]
     piece = total // group_size
     chunk = piece // (COLORS * PARTS)
     dma = pltpu.SemaphoreType.DMA
-    out, _ = pl.pallas_call(
+    any_spec = pl.BlockSpec(memory_space=pl.ANY)
+    out, _, vec, clip = pl.pallas_call(
         functools.partial(scatter_kernel, axis_name, piece),
         out_shape=(jax.ShapeDtypeStruct((1, piece), jnp.float32),
-                   jax.ShapeDtypeStruct((1, total // 2), jnp.bfloat16)),
-        in_specs=[pl.BlockSpec(memory_space=pl.ANY)],
-        out_specs=[pl.BlockSpec(memory_space=pl.ANY)] * 2,
+                   jax.ShapeDtypeStruct((1, total // 2), jnp.bfloat16),
+                   jax.ShapeDtypeStruct((1, n_vec), jnp.float32),
+                   jax.ShapeDtypeStruct((1, 128), jnp.float32)),
+        in_specs=[any_spec, any_spec],
+        out_specs=[any_spec, any_spec, any_spec, pl.BlockSpec(memory_space=pltpu.VMEM)],
         scratch_shapes=[
             pltpu.VMEM((2 * COLORS, 1, chunk), jnp.bfloat16),
             pltpu.VMEM((2 * COLORS, 1, chunk), jnp.bfloat16),
@@ -220,18 +292,135 @@
             pltpu.VMEM((4 * PARTS * COLORS, 1, chunk), jnp.float32),
             pltpu.VMEM((2 * PARTS * COLORS, 1, chunk), jnp.float32),
             pltpu.VMEM((PARTS * COLORS, 1, chunk), jnp.float32),
+            pltpu.VMEM((1, n_vec), jnp.bfloat16),
+            pltpu.VMEM((5, 1, n_vec), jnp.float32),
+            pltpu.VMEM((4, 1, n_vec), jnp.float32),
+            pltpu.VMEM((5, 1, 128), jnp.float32),
+            pltpu.VMEM((4, 1, 128), jnp.float32),
+            pltpu.VMEM((1, min(chunk, WIDTH)), jnp.float32),
             dma((2 * COLORS,)), dma((2 * COLORS,)),
             dma((4 * COLORS,)), dma((STEPS * COLORS,)),
             dma((3 * COLORS,)), dma((4 * PARTS * COLORS,)),
             dma((2 * PARTS * COLORS,)), dma((2 * PARTS * COLORS,)),
             dma((PARTS * COLORS,)), dma((PARTS * COLORS,)),
             dma((PARTS * COLORS,)),
+            dma, dma((4,)), dma((4,)), dma((4,)), dma((4,)), dma,
         ],
         compiler_params=pltpu.CompilerParams(
             collective_id=0, has_side_effects=True, vmem_limit_bytes=63 * 1024 * 1024),
         name="scatter_sum",
-    )(g_mat)
-    return out.reshape(piece)
+    )(g_mat, g_vec)
+    return out.reshape(piece), vec.reshape(n_vec), clip[0, 0]
+
+
+def gather_kernel(axis_name, x, out, s_sem, r_sem, own_sem, ds_sem, dr_sem):
+    own = COLORS * PARTS
+    me = lax.axis_index(axis_name)
+    deltas = [s * (1 - 2 * lax.rem(me // s, 2)) for s in STRIDES]
+    partner = me + 1 - 2 * lax.rem(me, 2)
+    peers = [me + d for d in deltas]
+
+    barrier = pltpu.get_barrier_semaphore()
+    for dev in (partner, *peers):
+        pl.semaphore_signal(barrier, inc=1, device_id=(dev,), device_id_type=MESH_ID)
+
+    def local(i):
+        return pltpu.make_async_copy(x.at[i], out.at[me * own + i], own_sem.at[i])
+
+    def across(src, index):
+        return pltpu.make_async_remote_copy(
+            src_ref=src, dst_ref=out.at[index], send_sem=ds_sem, recv_sem=dr_sem,
+            device_id=(partner,), device_id_type=MESH_ID)
+
+    def route(stage, axis):
+        b1, b2 = (axis - 2) % 3, (axis - 1) % 3
+        color = (axis, b2, b2, b1, b1, b1, b1)[stage]
+        flips = ((), (), (b2,), (), (b1,), (b2,), (b1, b2))[stage]
+        return color, sum((deltas[f] for f in flips), me), not flips
+
+    def push(stage, axis, q):
+        color, owner, mine = route(stage, axis)
+        index = owner * own + color * PARTS + q
+        k = (stage * 3 + axis) * PARTS + q
+        return pltpu.make_async_remote_copy(
+            src_ref=x.at[color * PARTS + q] if mine else out.at[index], dst_ref=out.at[index],
+            send_sem=s_sem.at[k], recv_sem=r_sem.at[k],
+            device_id=(peers[axis],), device_id_type=MESH_ID)
+
+    def land(stage, axis, q):
+        color, owner, _ = route(stage, axis)
+        index = (owner + deltas[axis]) * own + color * PARTS + q
+        push(stage, axis, q).wait_recv()
+        across(out.at[index], index).start()
+
+    def each(count, body):
+        lax.fori_loop(0, count, lambda i, c: (body(i), c)[1], 0)
+
+    pl.semaphore_wait(barrier, 4)
+
+    for stage in range(8):
+        def body(q, stage=stage):
+            for axis in range(3):
+                if stage < 7:
+                    push(stage, axis, q).start()
+                if stage:
+                    land(stage - 1, axis, q)
+                else:
+                    i = axis * PARTS + q
+                    across(x.at[i], me * own + i).start()
+        each(PARTS, body)
+        if stage == 0:
+            each(own, lambda i: local(i).start())
+
+    half = pltpu.make_async_remote_copy(
+        src_ref=out.at[pl.ds(0, 8 * own)], dst_ref=out.at[pl.ds(0, 8 * own)], send_sem=ds_sem, recv_sem=dr_sem,
+        device_id=(partner,), device_id_type=MESH_ID)
+    each(own, lambda i: local(i).wait())
+    for stage in range(7):
+        def body(q, stage=stage):
+            for axis in range(3):
+                push(stage, axis, q).wait_send()
+        each(PARTS, body)
+    half.wait_recv()
+    half.wait_send()
+
+
+def write_kernel(rows, held, out, sem):
+    def cut(ref, i):
+        return ref.at[pl.ds(i * rows, rows)]
+
+    copies = [pltpu.make_async_copy(cut(held, i), cut(out, i), sem.at[i]) for i in range(WRITES)]
+    for copy in copies:
+        copy.start()
+    for copy in copies:
+        copy.wait()
+
+
+def gather_params(piece_bf16, axis_name, group_size):
+    own = COLORS * PARTS
+    piece = piece_bf16.shape[0]
+    rows = piece // (own * 128)
+    dma = pltpu.SemaphoreType.DMA
+    full = pl.pallas_call(
+        functools.partial(gather_kernel, axis_name),
+        out_shape=pltpu.VMEM((group_size * own, rows, 128), jnp.bfloat16),
+        in_specs=[pl.BlockSpec(memory_space=pltpu.HBM)],
+        out_specs=pl.BlockSpec(memory_space=pltpu.VMEM),
+        scratch_shapes=[dma((7 * 3 * PARTS,)), dma((7 * 3 * PARTS,)), dma((own,)), dma, dma],
+        compiler_params=pltpu.CompilerParams(
+            collective_id=1, has_side_effects=True, vmem_limit_bytes=2 * 1024 * 1024),
+        name="gather_params",
+    )(piece_bf16.reshape(own, rows, 128))
+    full = pl.pallas_call(
+        functools.partial(write_kernel, group_size * own // WRITES),
+        out_shape=jax.ShapeDtypeStruct(full.shape, full.dtype),
+        in_specs=[pl.BlockSpec(memory_space=pltpu.VMEM)],
+        out_specs=pl.BlockSpec(memory_space=pl.ANY),
+        scratch_shapes=[dma((WRITES,))],
+        compiler_params=pltpu.CompilerParams(vmem_limit_bytes=1024 * 1024),
+        name="write_params",
+    )(full)
+    return full.reshape(group_size * piece)
 
 
 def solution(mesh):
@@ -239,13 +428,10 @@
     group_size = mesh.shape[axis_name]
 
     def local_step(g_mat, g_vec, p_mat, m_mat, v_mat, p_vec, m_vec, v_vec, learn_rate):
-        grad_mat = scatter_sum(g_mat, axis_name, group_size) / group_size
-        grad_vec = lax.psum(g_vec[0].astype(jnp.float32), axis_name) / group_size
-        norm_sq = lax.psum(jnp.sum(grad_mat * grad_mat), axis_name) + jnp.sum(grad_vec * grad_vec)
-        clip_scale = jnp.minimum(1.0, MAX_NORM / (jnp.sqrt(norm_sq) + NORM_EPS))
+        grad_mat, grad_vec, clip_scale = lax.optimization_barrier(scatter_sum(g_mat, g_vec, axis_name, group_size))
         new_p_mat, new_m_mat, new_v_mat = adam_update(grad_mat * clip_scale, p_mat, m_mat, v_mat, learn_rate, WEIGHT_DECAY)
         new_p_vec, new_m_vec, new_v_vec = adam_update(grad_vec * clip_scale, p_vec, m_vec, v_vec, learn_rate, 0.0)
-        full_params = lax.all_gather(new_p_mat.astype(jnp.bfloat16), axis_name, tiled=True)
+        full_params = gather_params(new_p_mat.astype(jnp.bfloat16), axis_name, group_size)
         return new_p_mat, new_m_mat, new_v_mat, new_p_vec, new_m_vec, new_v_vec, full_params
 
     return jax.shard_map(

time: 640 us -> 543 us (0.85)
  Pallas kernels: 334 us -> 523 us
  waiting for transfers between devices: 186 us -> 0 us
  local copies, waits for them, and re-layouts: 33.5 us -> 0.03 us
  blocking collectives: 31.9 us -> 0 us
  other arithmetic: 37.7 us -> 18.4 us
  between operations: 16.2 us -> 1.38 us
    all_gather x1 -> x0, waiting for transfers between devices: 186 us -> none  [local_step(): lax.all_gather(new_p_mat.astype(jnp.bfloat16), axis_name, tiled=True)]
    pallas_call x0 -> x2, Pallas kernels: none -> 179 us  [the longest x1 163 us: gather_params(): pl.pallas_call(functools.partial(gather_kernel, axis_name), out_shape=plt...]
    unnamed x9 -> x10, local copies, waits for them, and re-layouts: 33.5 us -> 0.03 us
    psum x1 -> x0, blocking collectives: 31.9 us -> none  [local_step(): lax.psum(jnp.sum(grad_mat * grad_mat), axis_name)]
    reduce_sum x2 -> x0, other arithmetic: 16.2 us -> none  [the longest x1 14.6 us: local_step(): jnp.sum(grad_mat * grad_mat)]
    pallas_call x1, Pallas kernels: 334 us -> 344 us  [scatter_sum(): pl.pallas_call(functools.partial(scatter_kernel, axis_name, piece), out_s...]
  transfers between devices with their start and end apart: 2 -> 0, of which waited for: 1 -> 0; matrix products, arithmetic and copies ran while one was open for 2% -> 0% of each run, Pallas kernels for 52% -> 0%
where the time goes in v2:
time: 543 us
  Pallas kernels  523 us (96%)
  other arithmetic  18.4 us (3%)
    pallas_call x1, Pallas kernels, scatter_sum(): pl.pallas_call(functools.partial(scatter_kernel, axis_name, piece), out_s...  344 us
    pallas_call x1, Pallas kernels, gather_params(): pl.pallas_call(functools.partial(gather_kernel, axis_name), out_shape=plt...  163 us
    convert_element_type x1, other arithmetic, local_step(): new_p_mat.astype(jnp.bfloat16)  17.6 us
    pallas_call x1, Pallas kernels, gather_params(): pl.pallas_call(functools.partial(write_kernel, group_size * own // WRITES...  16.2 us

profile of v2, /device:TPU:0, one launch (start us, length us, event | category | flops | bytes accessed | tf_op | source)
XLA Modules:
  0.0 543.1 jit_solution(16584803368581895913)
XLA Ops:
  0.6 344.4 %scatter_sum.1 = (f32[1,1572864]{1,0:T(1,128)}, bf16[1,12582912]{1,0:T(2,128)(2,1)}, f32[1,26624]{1,0:T(1,128)}, f32[1,128]{1,0:T(1,128)}) custom-call(bf16[1,25165824]{1,0:T(2,128)(2,1)} %g.1, bf16[1,26624]{1,0:T(2,128)(2,1)} %gv.1), custom_call_target="tpu_custom_call" | custom-call | tf_op jit(solution)/shard_map/scatter_sum/pallas_call | solution.py:280
  345.7 17.6 %fusion.2 = (bf16[1572864]{0:T(1024)(128)(2,1)S(1)}, f32[1572864]{0:T(1024)}, f32[1572864]{0:T(1024)}, f32[1572864]{0:T(1024)}) fusion(f32[1572864]{0:T(1024)} %param.11, f32[]{:T(128)S(6)} %copy.16, f32[1572864]{0:T(1024)} %bitcast.8, f32[]{:T(128)} %bitcast.10, f32[1572864]{0:T(1024)} %param.12, f32[1572864]{0:T(1024)} %param.13), kind=kLoop, calls=%fused_computation.8 | loop fusion | flops 26738688 | bytes 47185928 | tf_op jit(solution)/shard_map/convert_element_type | solution.py:434
  363.3 162.7 %gather_params.1.held = bf16[192,1024,128]{2,1,0:T(8,128)(2,1)S(1)} custom-call(bf16[12,1024,128]{2,1,0:T(8,128)(2,1)S(1)} %bitcast.6), custom_call_target="tpu_custom_call" | custom-call | tf_op jit(solution)/shard_map/gather_params/pallas_call | solution.py:404
  526.0 0.0 copy-start
  526.0 0.0 copy-start.1
  526.0 0.0 copy-start.2
  526.0 0.0 copy-start.3
  526.1 0.0 copy-start.4
  526.1 16.2 %write_params.1 = bf16[192,1024,128]{2,1,0:T(8,128)(2,1)} custom-call(bf16[192,1024,128]{2,1,0:T(8,128)(2,1)S(1)} %gather_params.1.held), custom_call_target="tpu_custom_call" | custom-call | tf_op jit(solution)/shard_map/write_params/pallas_call | solution.py:414
  542.2 0.0 copy-done
  542.3 0.0 copy-done.1
  542.3 0.0 copy-done.2
  542.3 0.0 copy-done.3
  542.3 0.0 copy-done.4
  542.3 0.8 multiply_subtract_fusion.1
Async XLA Ops:
  526.0 16.2 %copy-start = (f32[26624]{0:T(1024)S(1)}, f32[26624]{0:T(1024)}, u32[]{:S(2)}) copy-start(f32[26624]{0:T(1024)} %param.14) | copy-start | bytes 319492
  526.0 16.2 %copy-start.1 = (f32[26624]{0:T(1024)S(1)}, f32[26624]{0:T(1024)}, u32[]{:S(2)}) copy-start(f32[26624]{0:T(1024)} %param.15) | copy-start | bytes 319492
  526.0 16.2 %copy-start.2 = (f32[26624]{0:T(1024)S(1)}, f32[26624]{0:T(1024)}, u32[]{:S(2)}) copy-start(f32[26624]{0:T(1024)} %param.16) | copy-start | bytes 319492
  526.0 16.2 %copy-start.3 = (f32[1,26624]{1,0:T(1,128)S(1)}, f32[1,26624]{1,0:T(1,128)}, u32[]{:S(2)}) copy-start(f32[1,26624]{1,0:T(1,128)} %get-tuple-element.14) | copy-start | bytes 319492
  526.1 16.2 %copy-start.4 = (f32[1,128]{1,0:T(1,128)S(1)}, f32[1,128]{1,0:T(1,128)}, u32[]{:S(2)}) copy-start(f32[1,128]{1,0:T(1,128)} %get-tuple-element.15) | copy-start | bytes 1540

commit v3 on v2

--- a/solution.py
+++ b/solution.py
@@ -22,22 +22,18 @@
 PARTS = 4
 STRIDES = (2, 4, 8)
 STEPS = 8 * PARTS
+DEVICES = 16
 WIDTH = 4096
-WRITES = 16
+ROWS = 64
+SMALL_VMEM = 3400 * 1024
+RING = 5
 MEAN_SCALE = 1.0 / 16.0
 
 
-def adam_update(grad_vals, param_vals, moment_one, moment_two, learn_rate, decay_rate):
-    new_one = ADAM_BETA1 * moment_one + (1.0 - ADAM_BETA1) * grad_vals
-    new_two = ADAM_BETA2 * moment_two + (1.0 - ADAM_BETA2) * grad_vals * grad_vals
-    direction = (new_one / BIAS_ONE) / (jnp.sqrt(new_two / BIAS_TWO) + ADAM_EPS)
-    return param_vals - learn_rate * (direction + decay_rate * param_vals), new_one, new_two
-
-
-def scatter_kernel(axis_name, piece, g, gv, out, pg, vec_out, clip_out,
-                   a_buf, b_buf, stage, r1, r2, r3, v_in, v_acc, v_get, n_acc, n_get, squares,
+def scatter_kernel(axis_name, piece, g, gv, lr, out, pg, vec_out, scale_out,
+                   a_buf, b_buf, stage, r1, r2, r3, v_in, v_acc, v_get, n_put, n_get, squares, lr_smem, scale_buf,
                    a_sem, b_sem, ds_sem, dr_sem, s1_sem, r1_sem, s2_sem, r2_sem, s3_sem, r3_sem, o_sem,
-                   vi_sem, vs_sem, vr_sem, ns_sem, nr_sem, vo_sem):
+                   vi_sem, vs_sem, vr_sem, ns_sem, nr_sem, vo_sem, lr_sem, so_sem):
     chunk = piece // (COLORS * PARTS)
     width = min(chunk, WIDTH)
     n_vec = gv.shape[1]
@@ -122,8 +118,8 @@
 
     def norm_push(k):
         return pltpu.make_async_remote_copy(
-            src_ref=n_acc.at[k], dst_ref=n_get.at[k], send_sem=ns_sem.at[k], recv_sem=nr_sem.at[k],
-            device_id=((partner, *peers)[k],), device_id_type=MESH_ID)
+            src_ref=n_put, dst_ref=n_get.at[me], send_sem=ns_sem, recv_sem=nr_sem,
+            device_id=(lax.rem(me + k, DEVICES),), device_id_type=MESH_ID)
 
     def vec_loop(body):
         @pl.loop(0, n_vec // 1024)
@@ -156,6 +152,8 @@
             load_a(color, t).start()
     vec_load = pltpu.make_async_copy(gv, v_in, vi_sem)
     vec_load.start()
+    lr_load = pltpu.make_async_copy(lr, lr_smem, lr_sem)
+    lr_load.start()
     squares[...] = jnp.zeros_like(squares)
     pl.semaphore_wait(barrier, 4)
     for t in range(4):
@@ -244,13 +242,24 @@
     run(7 * PARTS, 7 * PARTS + 2, lambda t: phase_four(t, True))
     run(7 * PARTS + 2, STEPS, lambda t: phase_four(t, False))
 
-    n_acc[0] = jnp.broadcast_to(jnp.sum(squares[...], axis=1, keepdims=True), (1, 128))
-    for k in range(4):
+    part = jnp.broadcast_to(jnp.sum(squares[...], axis=1, keepdims=True), (1, 128))
+    n_put[...] = part
+    n_get[me] = part
+    for k in range(1, DEVICES):
         norm_push(k).start()
-        norm_push(k).wait_recv()
-        n_acc[k + 1] = n_acc[k] + n_get[k]
-    norm_sq = n_acc[4] + jnp.sum(v_get[0], axis=1, keepdims=True)
-    clip_out[...] = jnp.minimum(1.0, MAX_NORM / (jnp.sqrt(norm_sq) + NORM_EPS))
+    rest = pltpu.make_async_remote_copy(
+        src_ref=n_get.at[pl.ds(0, DEVICES - 1)], dst_ref=n_get.at[pl.ds(0, DEVICES - 1)],
+        send_sem=ns_sem, recv_sem=nr_sem, device_id=(partner,), device_id_type=MESH_ID)
+    rest.wait_recv()
+    norm_sq = n_get[0]
+    for k in range(1, DEVICES):
+        norm_sq = norm_sq + n_get[k]
+    norm_sq = norm_sq + jnp.sum(v_get[0], axis=1, keepdims=True)
+    scale_buf[0:1, :] = jnp.minimum(1.0, MAX_NORM / (jnp.sqrt(norm_sq) + NORM_EPS))
+    lr_load.wait()
+    scale_buf[1:2, :] = jnp.full((1, 128), lr_smem[0, 0])
+    scale_store = pltpu.make_async_copy(scale_buf, scale_out, so_sem)
+    scale_store.start()
 
     def drain(lo, hi, wait):
         def body(t):
@@ -263,28 +272,28 @@
     drain(6 * PARTS, 7 * PARTS, lambda c, t: push3(c, t).wait_send())
     drain(STEPS - 4, STEPS, lambda c, t: swap(c, t).wait_send())
     drain(7 * PARTS, STEPS, lambda c, t: store(c, t).wait())
-    for k in range(4):
-        norm_push(k).wait_send()
-        if k:
-            vec_push(k).wait_send()
+    for k in range(1, 4):
+        vec_push(k).wait_send()
+    rest.wait_send()
     vec_store.wait()
-
-
-def scatter_sum(g_mat, g_vec, axis_name, group_size):
+    scale_store.wait()
+
+
+def scatter_sum(g_mat, g_vec, learn_rate, axis_name, group_size):
     total = g_mat.shape[1]
     n_vec = g_vec.shape[1]
     piece = total // group_size
     chunk = piece // (COLORS * PARTS)
     dma = pltpu.SemaphoreType.DMA
     any_spec = pl.BlockSpec(memory_space=pl.ANY)
-    out, _, vec, clip = pl.pallas_call(
+    out, _, vec, scales = pl.pallas_call(
         functools.partial(scatter_kernel, axis_name, piece),
         out_shape=(jax.ShapeDtypeStruct((1, piece), jnp.float32),
                    jax.ShapeDtypeStruct((1, total // 2), jnp.bfloat16),
                    jax.ShapeDtypeStruct((1, n_vec), jnp.float32),
-                   jax.ShapeDtypeStruct((1, 128), jnp.float32)),
-        in_specs=[any_spec, any_spec],
-        out_specs=[any_spec, any_spec, any_spec, pl.BlockSpec(memory_space=pltpu.VMEM)],
+                   jax.ShapeDtypeStruct((2, 128), jnp.float32)),
+        in_specs=[any_spec] * 3,
+        out_specs=[any_spec] * 4,
         scratch_shapes=[
             pltpu.VMEM((2 * COLORS, 1, chunk), jnp.bfloat16),
             pltpu.VMEM((2 * COLORS, 1, chunk), jnp.bfloat16),
@@ -295,26 +304,42 @@
             pltpu.VMEM((1, n_vec), jnp.bfloat16),
             pltpu.VMEM((5, 1, n_vec), jnp.float32),
             pltpu.VMEM((4, 1, n_vec), jnp.float32),
-            pltpu.VMEM((5, 1, 128), jnp.float32),
-            pltpu.VMEM((4, 1, 128), jnp.float32),
+            pltpu.VMEM((1, 128), jnp.float32),
+            pltpu.VMEM((DEVICES, 1, 128), jnp.float32),
             pltpu.VMEM((1, min(chunk, WIDTH)), jnp.float32),
+            pltpu.SMEM((1, 1), jnp.float32),
+            pltpu.VMEM((2, 128), jnp.float32),
             dma((2 * COLORS,)), dma((2 * COLORS,)),
             dma((4 * COLORS,)), dma((STEPS * COLORS,)),
             dma((3 * COLORS,)), dma((4 * PARTS * COLORS,)),
             dma((2 * PARTS * COLORS,)), dma((2 * PARTS * COLORS,)),
             dma((PARTS * COLORS,)), dma((PARTS * COLORS,)),
             dma((PARTS * COLORS,)),
-            dma, dma((4,)), dma((4,)), dma((4,)), dma((4,)), dma,
+            dma, dma((4,)), dma((4,)), dma, dma, dma, dma, dma,
         ],
         compiler_params=pltpu.CompilerParams(
             collective_id=0, has_side_effects=True, vmem_limit_bytes=63 * 1024 * 1024),
         name="scatter_sum",
-    )(g_mat, g_vec)
-    return out.reshape(piece), vec.reshape(n_vec), clip[0, 0]
-
-
-def gather_kernel(axis_name, x, out, s_sem, r_sem, own_sem, ds_sem, dr_sem):
+    )(g_mat, g_vec, learn_rate.reshape(1, 1))
+    return out, vec, scales
+
+
+def adam_moments(grad, m, v):
+    new_m = ADAM_BETA1 * m + (1.0 - ADAM_BETA1) * grad
+    new_v = ADAM_BETA2 * v + (1.0 - ADAM_BETA2) * grad * grad
+    return new_m, new_v
+
+
+def adam_param(p, m, v, rate, decay):
+    direction = (m / BIAS_ONE) / (jnp.sqrt(v / BIAS_TWO) + ADAM_EPS)
+    return p - rate * (direction + decay * p)
+
+
+def gather_kernel(axis_name, grad, p, m, v, scales_in, out, m_out, v_out, g_buf, p_buf, scales,
+                  scales_sem, g_sem, p_sem, m_sem, v_sem, s_sem, r_sem, ds_sem, dr_sem):
     own = COLORS * PARTS
+    rows = p.shape[1]
+    step = min(rows, ROWS)
     me = lax.axis_index(axis_name)
     deltas = [s * (1 - 2 * lax.rem(me // s, 2)) for s in STRIDES]
     partner = me + 1 - 2 * lax.rem(me, 2)
@@ -324,103 +349,210 @@
     for dev in (partner, *peers):
         pl.semaphore_signal(barrier, inc=1, device_id=(dev,), device_id_type=MESH_ID)
 
-    def local(i):
-        return pltpu.make_async_copy(x.at[i], out.at[me * own + i], own_sem.at[i])
-
-    def across(src, index):
+    def loads(color, q):
+        i = color * PARTS + q
+        return (pltpu.make_async_copy(grad.at[i], g_buf.at[color], g_sem.at[color]),
+                pltpu.make_async_copy(m.at[i], m_out.at[i], m_sem.at[i]),
+                pltpu.make_async_copy(v.at[i], v_out.at[i], v_sem.at[i]),
+                pltpu.make_async_copy(p.at[i], p_buf.at[color], p_sem.at[color]))
+
+    def across(index):
         return pltpu.make_async_remote_copy(
-            src_ref=src, dst_ref=out.at[index], send_sem=ds_sem, recv_sem=dr_sem,
+            src_ref=out.at[index], dst_ref=out.at[index], send_sem=ds_sem, recv_sem=dr_sem,
             device_id=(partner,), device_id_type=MESH_ID)
 
     def route(stage, axis):
         b1, b2 = (axis - 2) % 3, (axis - 1) % 3
         color = (axis, b2, b2, b1, b1, b1, b1)[stage]
         flips = ((), (), (b2,), (), (b1,), (b2,), (b1, b2))[stage]
-        return color, sum((deltas[f] for f in flips), me), not flips
+        return color, sum((deltas[f] for f in flips), me)
 
     def push(stage, axis, q):
-        color, owner, mine = route(stage, axis)
+        color, owner = route(stage, axis)
         index = owner * own + color * PARTS + q
         k = (stage * 3 + axis) * PARTS + q
         return pltpu.make_async_remote_copy(
-            src_ref=x.at[color * PARTS + q] if mine else out.at[index], dst_ref=out.at[index],
-            send_sem=s_sem.at[k], recv_sem=r_sem.at[k],
+            src_ref=out.at[index], dst_ref=out.at[index], send_sem=s_sem.at[k], recv_sem=r_sem.at[k],
             device_id=(peers[axis],), device_id_type=MESH_ID)
 
     def land(stage, axis, q):
-        color, owner, _ = route(stage, axis)
-        index = (owner + deltas[axis]) * own + color * PARTS + q
+        color, owner = route(stage, axis)
         push(stage, axis, q).wait_recv()
-        across(out.at[index], index).start()
+        across((owner + deltas[axis]) * own + color * PARTS + q).start()
+
+    def update(color, q):
+        i = color * PARTS + q
+
+        @pl.loop(0, rows // step)
+        def _(r):
+            s = pl.ds(pl.multiple_of(r * step, step), step)
+            new_m, new_v = adam_moments(g_buf[color, s, :] * scales[0:1, :], m_out[i, s, :], v_out[i, s, :])
+            m_out[i, s, :] = new_m
+            v_out[i, s, :] = new_v
+            new_p = adam_param(p_buf[color, s, :], new_m, new_v, scales[1:2, :], WEIGHT_DECAY)
+            out[me * own + i, s, :] = new_p.astype(jnp.bfloat16)
 
     def each(count, body):
         lax.fori_loop(0, count, lambda i, c: (body(i), c)[1], 0)
 
-    pl.semaphore_wait(barrier, 4)
-
-    for stage in range(8):
+    scales_load = pltpu.make_async_copy(scales_in, scales, scales_sem)
+    scales_load.start()
+    for color in range(COLORS):
+        for copy in loads(color, 0):
+            copy.start()
+    scales_load.wait()
+    for q in range(PARTS):
+        for color in range(COLORS):
+            for copy in loads(color, q):
+                copy.wait()
+            update(color, q)
+            if q == 0 and color == 0:
+                pl.semaphore_wait(barrier, 4)
+            push(0, color, q).start()
+            push(1, (color + 1) % 3, q).start()
+            across(me * own + color * PARTS + q).start()
+            if q + 1 < PARTS:
+                for copy in loads(color, q + 1):
+                    copy.start()
+        if q >= 2:
+            for axis in range(3):
+                land(0, axis, q - 2)
+                land(1, axis, q - 2)
+    for q in range(PARTS):
+        for axis in range(3):
+            push(2, axis, q).start()
+            land(q % 2, axis, 2 + q // 2)
+    for stage in range(3, 8):
         def body(q, stage=stage):
             for axis in range(3):
                 if stage < 7:
                     push(stage, axis, q).start()
-                if stage:
-                    land(stage - 1, axis, q)
-                else:
-                    i = axis * PARTS + q
-                    across(x.at[i], me * own + i).start()
+                land(stage - 1, axis, q)
         each(PARTS, body)
-        if stage == 0:
-            each(own, lambda i: local(i).start())
-
-    half = pltpu.make_async_remote_copy(
-        src_ref=out.at[pl.ds(0, 8 * own)], dst_ref=out.at[pl.ds(0, 8 * own)], send_sem=ds_sem, recv_sem=dr_sem,
-        device_id=(partner,), device_id_type=MESH_ID)
-    each(own, lambda i: local(i).wait())
+
     for stage in range(7):
         def body(q, stage=stage):
             for axis in range(3):
                 push(stage, axis, q).wait_send()
         each(PARTS, body)
+    half = pltpu.make_async_remote_copy(
+        src_ref=out.at[pl.ds(0, 8 * own)], dst_ref=out.at[pl.ds(0, 8 * own)], send_sem=ds_sem, recv_sem=dr_sem,
+        device_id=(partner,), device_id_type=MESH_ID)
     half.wait_recv()
     half.wait_send()
 
 
-def write_kernel(rows, held, out, sem):
-    def cut(ref, i):
-        return ref.at[pl.ds(i * rows, rows)]
-
-    copies = [pltpu.make_async_copy(cut(held, i), cut(out, i), sem.at[i]) for i in range(WRITES)]
-    for copy in copies:
+def write_kernel(held, m_held, v_held, p, scales_in, g_vec, p_vec, m_vec, v_vec,
+                 out, p_out, m_out, v_out, pv_out, mv_out, vv_out,
+                 p_buf, vec_buf, scales, in_sem, out_sem, sem, vec_sem, vec_out_sem, scales_sem):
+    own, rows, _ = p.shape
+    step = min(rows, ROWS)
+    span = held.shape[0] // own
+
+    def load(i):
+        return pltpu.make_async_copy(p.at[i], p_buf.at[i % RING], in_sem.at[i % RING])
+
+    def store(i):
+        return pltpu.make_async_copy(p_buf.at[i % RING], p_out.at[i], out_sem.at[i % RING])
+
+    def copies(i):
+        part = pl.ds(i * span, span)
+        return (pltpu.make_async_copy(held.at[part], out.at[part], sem.at[0, i]),
+                pltpu.make_async_copy(m_held.at[i], m_out.at[i], sem.at[1, i]),
+                pltpu.make_async_copy(v_held.at[i], v_out.at[i], sem.at[2, i]))
+
+    scales_load = pltpu.make_async_copy(scales_in, scales, scales_sem)
+    scales_load.start()
+    vec_loads = [pltpu.make_async_copy(a, vec_buf.at[k], vec_sem.at[k])
+                 for k, a in enumerate((p_vec, m_vec, v_vec, g_vec))]
+    vec_stores = [pltpu.make_async_copy(vec_buf.at[k], a, vec_out_sem.at[k])
+                  for k, a in enumerate((pv_out, mv_out, vv_out))]
+    for i in range(RING - 1):
+        load(i).start()
+    for copy in vec_loads:
         copy.start()
-    for copy in copies:
+    for i in range(own):
+        for copy in copies(i):
+            copy.start()
+    scales_load.wait()
+    for i in range(own):
+        load(i).wait()
+
+        @pl.loop(0, rows // step)
+        def _(r):
+            s = pl.ds(pl.multiple_of(r * step, step), step)
+            p_buf[i % RING, s, :] = adam_param(
+                p_buf[i % RING, s, :], m_held[i, s, :], v_held[i, s, :], scales[1:2, :], WEIGHT_DECAY)
+
+        store(i).start()
+        if i + RING - 1 < own:
+            if i:
+                store(i - 1).wait()
+            load(i + RING - 1).start()
+    for copy in vec_loads:
         copy.wait()
 
-
-def gather_params(piece_bf16, axis_name, group_size):
+    @pl.loop(0, g_vec.shape[1] // 1024)
+    def _(i):
+        s = pl.ds(pl.multiple_of(i * 1024, 1024), 1024)
+        new_m, new_v = adam_moments(vec_buf[3, :, s] * scales[0:1, 0:1], vec_buf[1, :, s], vec_buf[2, :, s])
+        vec_buf[1, :, s] = new_m
+        vec_buf[2, :, s] = new_v
+        vec_buf[0, :, s] = adam_param(vec_buf[0, :, s], new_m, new_v, scales[1:2, 0:1], 0.0)
+
+    for copy in vec_stores:
+        copy.start()
+    for i in range(own - RING, own):
+        store(i).wait()
+    for i in range(own):
+        for copy in copies(i):
+            copy.wait()
+    for copy in vec_stores:
+        copy.wait()
+
+
+def gather_update(grad, p, m, v, scales, grad_vec, p_vec, m_vec, v_vec, axis_name, group_size):
     own = COLORS * PARTS
-    piece = piece_bf16.shape[0]
+    piece = p.shape[0]
+    n_vec = p_vec.shape[0]
     rows = piece // (own * 128)
     dma = pltpu.SemaphoreType.DMA
-    full = pl.pallas_call(
+    any_spec = pl.BlockSpec(memory_space=pl.ANY)
+    vmem_spec = pl.BlockSpec(memory_space=pltpu.VMEM)
+    grad, p, m, v = (a.reshape(own, rows, 128) for a in (grad, p, m, v))
+    p_vec, m_vec, v_vec = (a.reshape(1, n_vec) for a in (p_vec, m_vec, v_vec))
+    full, new_m, new_v = pl.pallas_call(
         functools.partial(gather_kernel, axis_name),
-        out_shape=pltpu.VMEM((group_size * own, rows, 128), jnp.bfloat16),
-        in_specs=[pl.BlockSpec(memory_space=pltpu.HBM)],
-        out_specs=pl.BlockSpec(memory_space=pltpu.VMEM),
-        scratch_shapes=[dma((7 * 3 * PARTS,)), dma((7 * 3 * PARTS,)), dma((own,)), dma, dma],
+        out_shape=(pltpu.VMEM((group_size * own, rows, 128), jnp.bfloat16),
+                   pltpu.VMEM((own, rows, 128), jnp.float32),
+                   pltpu.VMEM((own, rows, 128), jnp.float32)),
+        in_specs=[any_spec] * 5,
+        out_specs=[vmem_spec] * 3,
+        scratch_shapes=[
+            pltpu.VMEM((COLORS, rows, 128), jnp.float32), pltpu.VMEM((COLORS, rows, 128), jnp.float32),
+            pltpu.VMEM((2, 128), jnp.float32), dma, dma((COLORS,)), dma((COLORS,)), dma((own,)), dma((own,)),
+            dma((7 * 3 * PARTS,)), dma((7 * 3 * PARTS,)), dma, dma],
         compiler_params=pltpu.CompilerParams(
-            collective_id=1, has_side_effects=True, vmem_limit_bytes=2 * 1024 * 1024),
-        name="gather_params",
-    )(piece_bf16.reshape(own, rows, 128))
-    full = pl.pallas_call(
-        functools.partial(write_kernel, group_size * own // WRITES),
-        out_shape=jax.ShapeDtypeStruct(full.shape, full.dtype),
-        in_specs=[pl.BlockSpec(memory_space=pltpu.VMEM)],
-        out_specs=pl.BlockSpec(memory_space=pl.ANY),
-        scratch_shapes=[dma((WRITES,))],
-        compiler_params=pltpu.CompilerParams(vmem_limit_bytes=1024 * 1024),
-        name="write_params",
-    )(full)
-    return full.reshape(group_size * piece)
+            collective_id=1, has_side_effects=True, vmem_limit_bytes=SMALL_VMEM),
+        name="gather_update",
+    )(grad, p, m, v, scales)
+    flat = jax.ShapeDtypeStruct((own, rows, 128), jnp.float32)
+    line = jax.ShapeDtypeStruct((1, n_vec), jnp.float32)
+    full, new_p, new_m, new_v, *vecs = pl.pallas_call(
+        write_kernel,
+        out_shape=(jax.ShapeDtypeStruct(full.shape, full.dtype), flat, flat, flat, line, line, line),
+        in_specs=[vmem_spec] * 3 + [any_spec] * 6,
+        out_specs=[any_spec] * 7,
+        scratch_shapes=[
+            pltpu.VMEM((RING, rows, 128), jnp.float32), pltpu.VMEM((4, 1, n_vec), jnp.float32),
+            pltpu.VMEM((2, 128), jnp.float32),
+            dma((RING,)), dma((RING,)), dma((3, own)), dma((4,)), dma((3,)), dma],
+        compiler_params=pltpu.CompilerParams(vmem_limit_bytes=SMALL_VMEM),
+        name="write_out",
+    )(*(pltpu.with_memory_space_constraint(a, pltpu.VMEM) for a in (full, new_m, new_v)),
+      p, scales, grad_vec, p_vec, m_vec, v_vec)
+    return (*(a.reshape(piece) for a in (new_p, new_m, new_v)), *(a.reshape(n_vec) for a in vecs),
+            full.reshape(group_size * piece))
 
 
 def solution(mesh):
@@ -428,11 +560,8 @@
     group_size = mesh.shape[axis_name]
 
     def local_step(g_mat, g_vec, p_mat, m_mat, v_mat, p_vec, m_vec, v_vec, learn_rate):
-        grad_mat, grad_vec, clip_scale = lax.optimization_barrier(scatter_sum(g_mat, g_vec, axis_name, group_size))
-        new_p_mat, new_m_mat, new_v_mat = adam_update(grad_mat * clip_scale, p_mat, m_mat, v_mat, learn_rate, WEIGHT_DECAY)
-        new_p_vec, new_m_vec, new_v_vec = adam_update(grad_vec * clip_scale, p_vec, m_vec, v_vec, learn_rate, 0.0)
-        full_params = gather_params(new_p_mat.astype(jnp.bfloat16), axis_name, group_size)
-        return new_p_mat, new_m_mat, new_v_mat, new_p_vec, new_m_vec, new_v_vec, full_params
+        grad_mat, grad_vec, scales = scatter_sum(g_mat, g_vec, learn_rate, axis_name, group_size)
+        return gather_update(grad_mat, p_mat, m_mat, v_mat, scales, grad_vec, p_vec, m_vec, v_vec, axis_name, group_size)
 
     return jax.shard_map(
         local_step,

time: 543 us -> 535 us (0.985)
  other arithmetic: 18.4 us -> 0 us
  Pallas kernels: 523 us -> 534 us
    convert_element_type x1 -> x0, other arithmetic: 17.6 us -> none  [local_step(): new_p_mat.astype(jnp.bfloat16)]
    pallas_call x2, Pallas kernels: 179 us -> 195 us  [the longest x1 165 us: gather_update(): pl.pallas_call(functools.partial(gather_kernel, axis_name), out_shape=(pl...]
where the time goes in v3:
time: 535 us
  Pallas kernels  534 us (100%)
    pallas_call x1, Pallas kernels, scatter_sum(): pl.pallas_call(functools.partial(scatter_kernel, axis_name, piece), out_s...  339 us
    pallas_call x1, Pallas kernels, gather_update(): pl.pallas_call(functools.partial(gather_kernel, axis_name), out_shape=(pl...  165 us
    pallas_call x1, Pallas kernels, gather_update(): pl.pallas_call(write_kernel, out_shape=(jax.ShapeDtypeStruct(full.shape,...  29.6 us

profile of v3, /device:TPU:0, one launch (start us, length us, event | category | flops | bytes accessed | tf_op | source)
XLA Modules:
  0.0 535.2 jit_solution(4102114497377417200)
XLA Ops:
  1.3 339.2 %scatter_sum.1 = (f32[1,1572864]{1,0:T(1,128)}, bf16[1,12582912]{1,0:T(2,128)(2,1)}, f32[1,26624]{1,0:T(1,128)}, f32[2,128]{1,0:T(2,128)}) custom-call(bf16[1,25165824]{1,0:T(2,128)(2,1)} %g.1, bf16[1,26624]{1,0:T(2,128)(2,1)} %gv.1, f32[1,1]{1,0:T(1,128)} %bitcast.15.lr), custom_call_target="tpu_custom_call" | custom-call | tf_op jit(solution)/shard_map/scatter_sum/pallas_call | solution.py:289
  340.5 165.2 %gather_update.1 = (bf16[192,1024,128]{2,1,0:T(8,128)(2,1)S(1)}, f32[12,1024,128]{2,1,0:T(8,128)S(1)}, f32[12,1024,128]{2,1,0:T(8,128)S(1)}) custom-call(f32[12,1024,128]{2,1,0:T(8,128)} %bitcast.20, f32[12,1024,128]{2,1,0:T(8,128)} %bitcast.16, f32[12,1024,128]{2,1,0:T(8,128)} %bitcast.18, f32[12,1024,128]{2,1,0:T(8,128)} %bitcast.19, ...), custom_call_target="tpu_custom_call" | custom-call | tf_op jit(solution)/shard_map/gather_update/pallas_call | solution.py:524
  505.7 29.6 %write_out.1 = (bf16[192,1024,128]{2,1,0:T(8,128)(2,1)}, f32[12,1024,128]{2,1,0:T(8,128)}, f32[12,1024,128]{2,1,0:T(8,128)}, f32[12,1024,128]{2,1,0:T(8,128)}, f...) custom-call(bf16[192,1024,128]{2,1,0:T(8,128)(2,1)S(1)} %get-tuple-element.22.held, ...), custom_call_target="tpu_custom_call" | custom-call | tf_op jit(solution)/shard_map/write_out/pallas_call | solution.py:541

commit v4 on v3

--- a/solution.py
+++ b/solution.py
@@ -27,18 +27,23 @@
 ROWS = 64
 SMALL_VMEM = 3400 * 1024
 RING = 5
+AHEAD = 2
+CUTS = 4
 MEAN_SCALE = 1.0 / 16.0
 
 
 def scatter_kernel(axis_name, piece, g, gv, lr, out, pg, vec_out, scale_out,
-                   a_buf, b_buf, stage, r1, r2, r3, v_in, v_acc, v_get, n_put, n_get, squares, lr_smem, scale_buf,
-                   a_sem, b_sem, ds_sem, dr_sem, s1_sem, r1_sem, s2_sem, r2_sem, s3_sem, r3_sem, o_sem,
+                   a_buf, b_buf, stage, r1, r2, r3, v_in, v_full, v_acc, v_get, v_mean, n_put, n_get, squares, lr_smem, scale_buf,
+                   a_sem, b_sem, ds_sem, dr_sem, dc_sem, s1_sem, r1_sem, s2_sem, r2_sem, s3_sem, r3_sem, o_sem,
                    vi_sem, vs_sem, vr_sem, ns_sem, nr_sem, vo_sem, lr_sem, so_sem):
     chunk = piece // (COLORS * PARTS)
-    width = min(chunk, WIDTH)
+    width = min(chunk // CUTS, WIDTH)
+    part = chunk // CUTS
     n_vec = gv.shape[1]
+    n_half = n_vec // 2
     me = lax.axis_index(axis_name)
-    core_step = 1 - 2 * lax.rem(me, 2)
+    core = lax.rem(me, 2)
+    core_step = 1 - 2 * core
     deltas = [s * (1 - 2 * lax.rem(me // s, 2)) for s in STRIDES]
     partner = me + core_step
     peers = [me + d for d in deltas]
@@ -67,6 +72,25 @@
             recv_sem=dr_sem.at[color * STEPS + t],
             device_id=(partner,), device_id_type=MESH_ID)
 
+    def swap_early(color, t):
+        k = color * 2 + t
+        return pltpu.make_async_remote_copy(
+            src_ref=cut(g, offset(color, t) + core_step * piece), dst_ref=b_buf.at[k],
+            send_sem=ds_sem.at[color * 4 + t], recv_sem=dr_sem.at[color * STEPS + t],
+            device_id=(partner,), device_id_type=MESH_ID)
+
+    def swap_cut(color, i):
+        start = pl.multiple_of(offset(color, 0) + core_step * piece + i * part, 1024)
+        return pltpu.make_async_remote_copy(
+            src_ref=g.at[:, pl.ds(start, part)], dst_ref=b_buf.at[color * 2, :, pl.ds(i * part, part)],
+            send_sem=ds_sem.at[color * 4], recv_sem=dc_sem.at[color * CUTS + i],
+            device_id=(partner,), device_id_type=MESH_ID)
+
+    def push_cut(color, i):
+        k, j = color * 3, color * 4 * PARTS
+        s = pl.ds(i * part, part)
+        return push(stage.at[k, :, s], r1.at[j, :, s], s1_sem.at[k], r1_sem.at[j], color)
+
     def load_a(color, t):
         k = color * 2 + lax.rem(t, 2)
         return pltpu.make_async_copy(cut(g, offset(color, t)), a_buf.at[k], a_sem.at[k])
@@ -97,10 +121,11 @@
         j = color * PARTS + t - 7 * PARTS
         return pltpu.make_async_copy(r3.at[j], cut(out, j * chunk), o_sem.at[j])
 
-    def add_up(color, t, dst, extra, last=False):
+    def add_up(color, t, dst, extra, last=False, span=None):
         k = color * 2 + lax.rem(t, 2)
-
-        @pl.loop(0, chunk // width)
+        first, count = span or (0, chunk)
+
+        @pl.loop(first // width, (first + count) // width)
         def _(i):
             s = pl.ds(pl.multiple_of(i * width, width), width)
             acc = a_buf[k, :, s].astype(jnp.float32) + b_buf[k, :, s].astype(jnp.float32)
@@ -111,28 +136,38 @@
                 squares[...] += acc * acc
             dst[0][dst[1], :, s] = acc
 
+    def half(ref, which):
+        return ref.at[:, pl.ds(pl.multiple_of(which * n_half, 1024), n_half)]
+
     def vec_push(k):
-        return pltpu.make_async_remote_copy(
-            src_ref=v_acc.at[k], dst_ref=v_get.at[k], send_sem=vs_sem.at[k], recv_sem=vr_sem.at[k],
-            device_id=((partner, *peers)[k],), device_id_type=MESH_ID)
+        src = half(v_full, 1 - core) if k == 0 else half(v_mean, core) if k == 4 else v_acc.at[k]
+        return pltpu.make_async_remote_copy(
+            src_ref=src, dst_ref=half(v_mean, core) if k == 4 else v_get.at[k],
+            send_sem=vs_sem.at[k], recv_sem=vr_sem.at[k],
+            device_id=((partner, *peers, partner)[k],), device_id_type=MESH_ID)
 
     def norm_push(k):
         return pltpu.make_async_remote_copy(
             src_ref=n_put, dst_ref=n_get.at[me], send_sem=ns_sem, recv_sem=nr_sem,
             device_id=(lax.rem(me + k, DEVICES),), device_id_type=MESH_ID)
 
-    def vec_loop(body):
-        @pl.loop(0, n_vec // 1024)
+    def vec_loop(count, body):
+        @pl.loop(0, count // 1024)
         def _(i):
-            body(pl.ds(pl.multiple_of(i * 1024, 1024), 1024))
+            body(pl.multiple_of(i * 1024, 1024))
 
     def vec_turn(k):
-        def body(s):
-            v_acc[k + 1, :, s] = v_acc[k, :, s] + v_get[k, :, s]
+        def body(i):
+            s = pl.ds(i, 1024)
+            here = pl.ds(pl.multiple_of(core * n_half + i, 1024), 1024)
+            total = (v_acc[k, :, s] if k else v_full[:, here]) + v_get[k, :, s]
+            if k < 3:
+                v_acc[k + 1, :, s] = total
+            else:
+                v_mean[:, here] = total * MEAN_SCALE
         vec_push(k).wait_recv()
-        vec_loop(body)
-        if k < 3:
-            vec_push(k + 1).start()
+        vec_loop(n_half, body)
+        vec_push(k + 1).start()
 
     def ready(color, t):
         load_a(color, t).wait()
@@ -156,17 +191,32 @@
     lr_load.start()
     squares[...] = jnp.zeros_like(squares)
     pl.semaphore_wait(barrier, 4)
-    for t in range(4):
+    for i in range(CUTS):
+        for color in range(COLORS):
+            swap_cut(color, i).start()
+    for color in range(COLORS):
+        swap_early(color, 1).start()
+    for t in range(2, 4):
         for color in range(COLORS):
             swap(color, t).start()
-    for t in range(2):
-        for color in range(COLORS):
-            swap(color, t).wait_recv()
-            load_b(color, t).start()
-
-    def phase_one(t, first):
-        for color in range(COLORS):
-            ready(color, t)
+    for i in range(CUTS):
+        for color in range(COLORS):
+            if i == 0:
+                load_a(color, 0).wait()
+            swap_cut(color, i).wait_recv()
+            add_up(color, 0, (stage, color * 3), (), span=(i * part, part))
+            push_cut(color, i).start()
+    for color in range(COLORS):
+        more_swap(color, 4)
+        refill(color, 2)
+
+    def phase_one(t, first, early=False):
+        for color in range(COLORS):
+            if early:
+                load_a(color, t).wait()
+                swap_early(color, t).wait_recv()
+            else:
+                ready(color, t)
             if not first:
                 push1(color, t - 3).wait_send()
             add_up(color, t, (stage, color * 3 + lax.rem(t, 3)), ())
@@ -177,27 +227,22 @@
     def run(lo, hi, body):
         lax.fori_loop(lo, hi, lambda t, c: (body(t), c)[1], 0)
 
-    run(0, 3, lambda t: phase_one(t, True))
+    phase_one(1, True, True)
+    phase_one(2, True)
     vec_load.wait()
 
-    def widen(s):
-        v_acc[0, :, s] = v_in[:, s].astype(jnp.float32)
-
-    vec_loop(widen)
+    def widen(i):
+        s = pl.ds(i, 1024)
+        v_full[:, s] = v_in[:, s].astype(jnp.float32)
+
+    vec_loop(n_vec, widen)
     vec_push(0).start()
     for k in range(4):
         run(3 * k + 3, 3 * k + 6, lambda t: phase_one(t, False))
         vec_turn(k)
     run(15, 4 * PARTS, lambda t: phase_one(t, False))
-
-    def vec_mean(s):
-        mean = v_acc[4, :, s] * MEAN_SCALE
-        v_acc[0, :, s] = mean
-        v_get[0, :, s] = mean * mean
-
-    vec_push(0).wait_send()
-    vec_loop(vec_mean)
-    vec_store = pltpu.make_async_copy(v_acc.at[0], vec_out, vo_sem)
+    vec_push(4).wait_recv()
+    vec_store = pltpu.make_async_copy(v_mean, vec_out, vo_sem)
     vec_store.start()
 
     def phase_two(t):
@@ -242,9 +287,10 @@
     run(7 * PARTS, 7 * PARTS + 2, lambda t: phase_four(t, True))
     run(7 * PARTS + 2, STEPS, lambda t: phase_four(t, False))
 
-    part = jnp.broadcast_to(jnp.sum(squares[...], axis=1, keepdims=True), (1, 128))
-    n_put[...] = part
-    n_get[me] = part
+    vec_sq = jnp.sum(v_mean[...] * v_mean[...], axis=1, keepdims=True)
+    mine = jnp.broadcast_to(jnp.sum(squares[...], axis=1, keepdims=True), (1, 128))
+    n_put[...] = mine
+    n_get[me] = mine
     for k in range(1, DEVICES):
         norm_push(k).start()
     rest = pltpu.make_async_remote_copy(
@@ -254,7 +300,7 @@
     norm_sq = n_get[0]
     for k in range(1, DEVICES):
         norm_sq = norm_sq + n_get[k]
-    norm_sq = norm_sq + jnp.sum(v_get[0], axis=1, keepdims=True)
+    norm_sq = norm_sq + vec_sq
     scale_buf[0:1, :] = jnp.minimum(1.0, MAX_NORM / (jnp.sqrt(norm_sq) + NORM_EPS))
     lr_load.wait()
     scale_buf[1:2, :] = jnp.full((1, 128), lr_smem[0, 0])
@@ -272,7 +318,7 @@
     drain(6 * PARTS, 7 * PARTS, lambda c, t: push3(c, t).wait_send())
     drain(STEPS - 4, STEPS, lambda c, t: swap(c, t).wait_send())
     drain(7 * PARTS, STEPS, lambda c, t: store(c, t).wait())
-    for k in range(1, 4):
+    for k in range(5):
         vec_push(k).wait_send()
     rest.wait_send()
     vec_store.wait()
@@ -302,20 +348,22 @@
             pltpu.VMEM((2 * PARTS * COLORS, 1, chunk), jnp.float32),
             pltpu.VMEM((PARTS * COLORS, 1, chunk), jnp.float32),
             pltpu.VMEM((1, n_vec), jnp.bfloat16),
-            pltpu.VMEM((5, 1, n_vec), jnp.float32),
-            pltpu.VMEM((4, 1, n_vec), jnp.float32),
+            pltpu.VMEM((1, n_vec), jnp.float32),
+            pltpu.VMEM((4, 1, n_vec // 2), jnp.float32),
+            pltpu.VMEM((4, 1, n_vec // 2), jnp.float32),
+            pltpu.VMEM((1, n_vec), jnp.float32),
             pltpu.VMEM((1, 128), jnp.float32),
             pltpu.VMEM((DEVICES, 1, 128), jnp.float32),
-            pltpu.VMEM((1, min(chunk, WIDTH)), jnp.float32),
+            pltpu.VMEM((1, min(chunk // CUTS, WIDTH)), jnp.float32),
             pltpu.SMEM((1, 1), jnp.float32),
             pltpu.VMEM((2, 128), jnp.float32),
             dma((2 * COLORS,)), dma((2 * COLORS,)),
-            dma((4 * COLORS,)), dma((STEPS * COLORS,)),
+            dma((4 * COLORS,)), dma((STEPS * COLORS,)), dma((CUTS * COLORS,)),
             dma((3 * COLORS,)), dma((4 * PARTS * COLORS,)),
             dma((2 * PARTS * COLORS,)), dma((2 * PARTS * COLORS,)),
             dma((PARTS * COLORS,)), dma((PARTS * COLORS,)),
             dma((PARTS * COLORS,)),
-            dma, dma((4,)), dma((4,)), dma, dma, dma, dma, dma,
+            dma, dma((5,)), dma((5,)), dma, dma, dma, dma, dma,
         ],
         compiler_params=pltpu.CompilerParams(
             collective_id=0, has_side_effects=True, vmem_limit_bytes=63 * 1024 * 1024),
@@ -467,11 +515,26 @@
                  for k, a in enumerate((p_vec, m_vec, v_vec, g_vec))]
     vec_stores = [pltpu.make_async_copy(vec_buf.at[k], a, vec_out_sem.at[k])
                   for k, a in enumerate((pv_out, mv_out, vv_out))]
+    def vec_update():
+        for copy in vec_loads:
+            copy.wait()
+
+        @pl.loop(0, g_vec.shape[1] // 1024)
+        def _(i):
+            s = pl.ds(pl.multiple_of(i * 1024, 1024), 1024)
+            new_m, new_v = adam_moments(vec_buf[3, :, s] * scales[0:1, 0:1], vec_buf[1, :, s], vec_buf[2, :, s])
+            vec_buf[1, :, s] = new_m
+            vec_buf[2, :, s] = new_v
+            vec_buf[0, :, s] = adam_param(vec_buf[0, :, s], new_m, new_v, scales[1:2, 0:1], 0.0)
+
+        for copy in vec_stores:
+            copy.start()
+
     for i in range(RING - 1):
         load(i).start()
     for copy in vec_loads:
         copy.start()
-    for i in range(own):
+    for i in range(AHEAD):
         for copy in copies(i):
             copy.start()
     scales_load.wait()
@@ -489,22 +552,17 @@
             if i:
                 store(i - 1).wait()
             load(i + RING - 1).start()
-    for copy in vec_loads:
-        copy.wait()
-
-    @pl.loop(0, g_vec.shape[1] // 1024)
-    def _(i):
-        s = pl.ds(pl.multiple_of(i * 1024, 1024), 1024)
-        new_m, new_v = adam_moments(vec_buf[3, :, s] * scales[0:1, 0:1], vec_buf[1, :, s], vec_buf[2, :, s])
-        vec_buf[1, :, s] = new_m
-        vec_buf[2, :, s] = new_v
-        vec_buf[0, :, s] = adam_param(vec_buf[0, :, s], new_m, new_v, scales[1:2, 0:1], 0.0)
-
-    for copy in vec_stores:
-        copy.start()
+        if i + AHEAD < own:
+            for copy in copies(i):
+                copy.wait()
+            for copy in copies(i + AHEAD):
+                copy.start()
+        if i == 0:
+            vec_update()
+
     for i in range(own - RING, own):
         store(i).wait()
-    for i in range(own):
+    for i in range(own - AHEAD, own):
         for copy in copies(i):
             copy.wait()
     for copy in vec_stores:

time: 535 us -> 523 us (0.978)
  Pallas kernels: 534 us -> 522 us
    pallas_call x1, Pallas kernels: 339 us -> 332 us  [scatter_sum(): pl.pallas_call(functools.partial(scatter_kernel, axis_name, piece), out_s...]
where the time goes in v4:
time: 523 us
  Pallas kernels  522 us (100%)
    pallas_call x1, Pallas kernels, scatter_sum(): pl.pallas_call(functools.partial(scatter_kernel, axis_name, piece), out_s...  332 us
    pallas_call x1, Pallas kernels, gather_update(): pl.pallas_call(functools.partial(gather_kernel, axis_name), out_shape=(pl...  165 us
    pallas_call x1, Pallas kernels, gather_update(): pl.pallas_call(write_kernel, out_shape=(jax.ShapeDtypeStruct(full.shape,...  24.3 us

profile of v4, /device:TPU:0, one launch (start us, length us, event | category | flops | bytes accessed | tf_op | source)
XLA Modules:
  0.0 523.0 jit_solution(12879868929753506596)
XLA Ops:
  1.3 332.3 %scatter_sum.1 = (f32[1,1572864]{1,0:T(1,128)}, bf16[1,12582912]{1,0:T(2,128)(2,1)}, f32[1,26624]{1,0:T(1,128)}, f32[2,128]{1,0:T(2,128)}) custom-call(bf16[1,25165824]{1,0:T(2,128)(2,1)} %g.1, bf16[1,26624]{1,0:T(2,128)(2,1)} %gv.1, f32[1,1]{1,0:T(1,128)} %bitcast.15.lr), custom_call_target="tpu_custom_call" | custom-call | tf_op jit(solution)/shard_map/scatter_sum/pallas_call | solution.py:335
  333.5 165.2 %gather_update.1 = (bf16[192,1024,128]{2,1,0:T(8,128)(2,1)S(1)}, f32[12,1024,128]{2,1,0:T(8,128)S(1)}, f32[12,1024,128]{2,1,0:T(8,128)S(1)}) custom-call(f32[12,1024,128]{2,1,0:T(8,128)} %bitcast.20, f32[12,1024,128]{2,1,0:T(8,128)} %bitcast.16, f32[12,1024,128]{2,1,0:T(8,128)} %bitcast.18, f32[12,1024,128]{2,1,0:T(8,128)} %bitcast.19, ...), custom_call_target="tpu_custom_call" | custom-call | tf_op jit(solution)/shard_map/gather_update/pallas_call | solution.py:582
  498.7 24.3 %write_out.1 = (bf16[192,1024,128]{2,1,0:T(8,128)(2,1)}, f32[12,1024,128]{2,1,0:T(8,128)}, f32[12,1024,128]{2,1,0:T(8,128)}, f32[12,1024,128]{2,1,0:T(8,128)}, f...) custom-call(bf16[192,1024,128]{2,1,0:T(8,128)(2,1)S(1)} %get-tuple-element.22.held, ...), custom_call_target="tpu_custom_call" | custom-call | tf_op jit(solution)/shard_map/write_out/pallas_call | solution.py:599

commit v5 on v4

--- a/solution.py
+++ b/solution.py
@@ -33,8 +33,8 @@
 
 
 def scatter_kernel(axis_name, piece, g, gv, lr, out, pg, vec_out, scale_out,
-                   a_buf, b_buf, stage, r1, r2, r3, v_in, v_full, v_acc, v_get, v_mean, n_put, n_get, squares, lr_smem, scale_buf,
-                   a_sem, b_sem, ds_sem, dr_sem, dc_sem, s1_sem, r1_sem, s2_sem, r2_sem, s3_sem, r3_sem, o_sem,
+                   a_buf, b_buf, e_buf, stage, r1, r2, r3, v_in, v_full, v_acc, v_get, v_mean, n_put, n_get, squares, lr_smem, scale_buf,
+                   a_sem, b_sem, e_sem, ds_sem, dr_sem, dc_sem, s1_sem, r1_sem, s2_sem, r2_sem, s3_sem, r3_sem, rc_sem, o_sem,
                    vi_sem, vs_sem, vr_sem, ns_sem, nr_sem, vo_sem, lr_sem, so_sem):
     chunk = piece // (COLORS * PARTS)
     width = min(chunk // CUTS, WIDTH)
@@ -69,27 +69,31 @@
             src_ref=cut(g, offset(color, t) + core_step * piece),
             dst_ref=cut(pg, (color * STEPS + t) * chunk),
             send_sem=ds_sem.at[color * 4 + lax.rem(t, 4)],
-            recv_sem=dr_sem.at[color * STEPS + t],
+            recv_sem=dr_sem.at[color * 8 + lax.rem(t, 8)],
             device_id=(partner,), device_id_type=MESH_ID)
 
     def swap_early(color, t):
         k = color * 2 + t
         return pltpu.make_async_remote_copy(
             src_ref=cut(g, offset(color, t) + core_step * piece), dst_ref=b_buf.at[k],
-            send_sem=ds_sem.at[color * 4 + t], recv_sem=dr_sem.at[color * STEPS + t],
+            send_sem=ds_sem.at[color * 4 + t], recv_sem=dr_sem.at[color * 8 + t],
             device_id=(partner,), device_id_type=MESH_ID)
 
     def swap_cut(color, i):
-        start = pl.multiple_of(offset(color, 0) + core_step * piece + i * part, 1024)
-        return pltpu.make_async_remote_copy(
-            src_ref=g.at[:, pl.ds(start, part)], dst_ref=b_buf.at[color * 2, :, pl.ds(i * part, part)],
+        s = pl.ds(i * part, part)
+        return pltpu.make_async_remote_copy(
+            src_ref=e_buf.at[color, :, s], dst_ref=b_buf.at[color * 2, :, s],
             send_sem=ds_sem.at[color * 4], recv_sem=dc_sem.at[color * CUTS + i],
             device_id=(partner,), device_id_type=MESH_ID)
+
+    def load_e(color):
+        return pltpu.make_async_copy(
+            cut(g, offset(color, 0) + core_step * piece), e_buf.at[color], e_sem.at[color])
 
     def push_cut(color, i):
         k, j = color * 3, color * 4 * PARTS
         s = pl.ds(i * part, part)
-        return push(stage.at[k, :, s], r1.at[j, :, s], s1_sem.at[k], r1_sem.at[j], color)
+        return push(stage.at[k, :, s], r1.at[j, :, s], s1_sem.at[k], r1_sem.at[color * 4], color)
 
     def load_a(color, t):
         k = color * 2 + lax.rem(t, 2)
@@ -107,19 +111,33 @@
     def push1(color, t):
         k = color * 3 + lax.rem(t, 3)
         j = color * 4 * PARTS + t
-        return push(stage.at[k], r1.at[j], s1_sem.at[k], r1_sem.at[j], color)
+        return push(stage.at[k], r1.at[j], s1_sem.at[k], r1_sem.at[color * 4 + t // PARTS], color)
 
     def push2(color, t):
         j = color * 2 * PARTS + t - 4 * PARTS
-        return push(r1.at[color * 4 * PARTS + t - 4 * PARTS], r2.at[j], s2_sem.at[j], r2_sem.at[j], (color + 1) % 3)
+        return push(r1.at[color * 4 * PARTS + t - 4 * PARTS], r2.at[j], s2_sem,
+                    r2_sem.at[color * 2 + t // PARTS - 4], (color + 1) % 3)
 
     def push3(color, t):
         j = color * PARTS + t - 6 * PARTS
-        return push(r1.at[color * 4 * PARTS + t - 4 * PARTS], r3.at[j], s3_sem.at[j], r3_sem.at[j], (color + 2) % 3)
+        return push(r1.at[color * 4 * PARTS + t - 4 * PARTS], r3.at[j], s3_sem, r3_sem.at[j], (color + 2) % 3)
+
+    def push3_cut(color, i):
+        s = pl.ds(i * part, part)
+        return push(r1.at[color * 4 * PARTS + 3 * PARTS - 1, :, s], r3.at[color * PARTS + PARTS - 1, :, s],
+                    s3_sem, rc_sem.at[color * CUTS + i], (color + 2) % 3)
+
+    def unit1(color, u):
+        span = r1.at[pl.ds((color * 4 + u) * PARTS, PARTS)]
+        return push(span, span, s2_sem, r1_sem.at[color * 4 + u], color)
+
+    def unit2(color, w):
+        span = r2.at[pl.ds((color * 2 + w) * PARTS, PARTS)]
+        return push(span, span, s2_sem, r2_sem.at[color * 2 + w], (color + 1) % 3)
 
     def store(color, t):
         j = color * PARTS + t - 7 * PARTS
-        return pltpu.make_async_copy(r3.at[j], cut(out, j * chunk), o_sem.at[j])
+        return pltpu.make_async_copy(r3.at[j], cut(out, j * chunk), o_sem)
 
     def add_up(color, t, dst, extra, last=False, span=None):
         k = color * 2 + lax.rem(t, 2)
@@ -182,6 +200,8 @@
         swap(color, t - 4).wait_send()
         swap(color, t).start()
 
+    for color in range(COLORS):
+        load_e(color).start()
     for t in range(2):
         for color in range(COLORS):
             load_a(color, t).start()
@@ -190,6 +210,8 @@
     lr_load = pltpu.make_async_copy(lr, lr_smem, lr_sem)
     lr_load.start()
     squares[...] = jnp.zeros_like(squares)
+    for color in range(COLORS):
+        load_e(color).wait()
     pl.semaphore_wait(barrier, 4)
     for i in range(CUTS):
         for color in range(COLORS):
@@ -249,43 +271,62 @@
         for color in range(COLORS):
             ready(color, t)
             j = color * 4 * PARTS + t - 4 * PARTS
-            push1(color, t - 4 * PARTS).wait_recv()
             add_up(color, t, (r1, j), ((r1, j),))
             push2(color, t).start()
             more_swap(color, t + 4)
             refill(color, t + 2)
 
-    run(4 * PARTS, 6 * PARTS, phase_two)
-
-    def phase_three(t):
+    def phase_three(t, cuts):
         for color in range(COLORS):
             ready(color, t)
             j = color * 4 * PARTS + t - 4 * PARTS
-            push1(color, t - 4 * PARTS).wait_recv()
-            push2(color, t - 2 * PARTS).wait_recv()
             add_up(color, t, (r1, j), ((r1, j), (r2, color * 2 * PARTS + t - 6 * PARTS)))
-            push3(color, t).start()
+            if cuts:
+                for i in range(CUTS):
+                    push3_cut(color, i).start()
+            else:
+                push3(color, t).start()
             more_swap(color, t + 4)
             refill(color, t + 2)
 
-    run(6 * PARTS, 7 * PARTS, phase_three)
+    def finish(color, t, span=None):
+        j = color * PARTS + t - 7 * PARTS
+        add_up(color, t, (r3, j), (
+            (r1, color * 4 * PARTS + t - 4 * PARTS),
+            (r2, color * 2 * PARTS + t - 6 * PARTS),
+            (r3, j)), last=True, span=span)
 
     def phase_four(t, fill):
         for color in range(COLORS):
             ready(color, t)
-            push1(color, t - 4 * PARTS).wait_recv()
-            push2(color, t - 2 * PARTS).wait_recv()
             push3(color, t - PARTS).wait_recv()
-            add_up(color, t, (r3, color * PARTS + t - 7 * PARTS), (
-                (r1, color * 4 * PARTS + t - 4 * PARTS),
-                (r2, color * 2 * PARTS + t - 6 * PARTS),
-                (r3, color * PARTS + t - 7 * PARTS)), last=True)
+            finish(color, t)
             store(color, t).start()
             if fill:
                 refill(color, t + 2)
 
-    run(7 * PARTS, 7 * PARTS + 2, lambda t: phase_four(t, True))
-    run(7 * PARTS + 2, STEPS, lambda t: phase_four(t, False))
+    for unit in range(4, 8):
+        for color in range(COLORS):
+            unit1(color, unit - 4).wait_recv()
+            if unit >= 6:
+                unit2(color, unit - 6).wait_recv()
+        lo = unit * PARTS
+        if unit < 6:
+            run(lo, lo + PARTS, phase_two)
+        elif unit == 6:
+            run(lo, lo + PARTS - 1, lambda t: phase_three(t, False))
+            phase_three(lo + PARTS - 1, True)
+        else:
+            run(lo, lo + PARTS - 2, lambda t: phase_four(t, True))
+            phase_four(lo + PARTS - 2, False)
+    for color in range(COLORS):
+        ready(color, STEPS - 1)
+    for i in range(CUTS):
+        for color in range(COLORS):
+            push3_cut(color, i).wait_recv()
+            finish(color, STEPS - 1, span=(i * part, part))
+    for color in range(COLORS):
+        store(color, STEPS - 1).start()
 
     vec_sq = jnp.sum(v_mean[...] * v_mean[...], axis=1, keepdims=True)
     mine = jnp.broadcast_to(jnp.sum(squares[...], axis=1, keepdims=True), (1, 128))
@@ -303,7 +344,7 @@
     norm_sq = norm_sq + vec_sq
     scale_buf[0:1, :] = jnp.minimum(1.0, MAX_NORM / (jnp.sqrt(norm_sq) + NORM_EPS))
     lr_load.wait()
-    scale_buf[1:2, :] = jnp.full((1, 128), lr_smem[0, 0])
+    scale_buf[1:2, :] = jnp.full((1, 128), lr_smem[0])
     scale_store = pltpu.make_async_copy(scale_buf, scale_out, so_sem)
     scale_store.start()
 
@@ -314,10 +355,10 @@
         run(lo, hi, body)
 
     drain(4 * PARTS - 3, 4 * PARTS, lambda c, t: push1(c, t).wait_send())
-    drain(4 * PARTS, 6 * PARTS, lambda c, t: push2(c, t).wait_send())
-    drain(6 * PARTS, 7 * PARTS, lambda c, t: push3(c, t).wait_send())
+    push(r2, r2, s2_sem, r2_sem.at[0], 0).wait_send()
+    push(r3, r3, s3_sem, r3_sem.at[0], 0).wait_send()
     drain(STEPS - 4, STEPS, lambda c, t: swap(c, t).wait_send())
-    drain(7 * PARTS, STEPS, lambda c, t: store(c, t).wait())
+    pltpu.make_async_copy(out, out, o_sem).wait()
     for k in range(5):
         vec_push(k).wait_send()
     rest.wait_send()
@@ -343,6 +384,7 @@
         scratch_shapes=[
             pltpu.VMEM((2 * COLORS, 1, chunk), jnp.bfloat16),
             pltpu.VMEM((2 * COLORS, 1, chunk), jnp.bfloat16),
+            pltpu.VMEM((COLORS, 1, chunk), jnp.bfloat16),
             pltpu.VMEM((3 * COLORS, 1, chunk), jnp.float32),
             pltpu.VMEM((4 * PARTS * COLORS, 1, chunk), jnp.float32),
             pltpu.VMEM((2 * PARTS * COLORS, 1, chunk), jnp.float32),
@@ -355,20 +397,18 @@
             pltpu.VMEM((1, 128), jnp.float32),
             pltpu.VMEM((DEVICES, 1, 128), jnp.float32),
             pltpu.VMEM((1, min(chunk // CUTS, WIDTH)), jnp.float32),
-            pltpu.SMEM((1, 1), jnp.float32),
+            pltpu.SMEM((1,), jnp.float32),
             pltpu.VMEM((2, 128), jnp.float32),
-            dma((2 * COLORS,)), dma((2 * COLORS,)),
-            dma((4 * COLORS,)), dma((STEPS * COLORS,)), dma((CUTS * COLORS,)),
-            dma((3 * COLORS,)), dma((4 * PARTS * COLORS,)),
-            dma((2 * PARTS * COLORS,)), dma((2 * PARTS * COLORS,)),
-            dma((PARTS * COLORS,)), dma((PARTS * COLORS,)),
-            dma((PARTS * COLORS,)),
+            dma((2 * COLORS,)), dma((2 * COLORS,)), dma((COLORS,)),
+            dma((4 * COLORS,)), dma((8 * COLORS,)), dma((CUTS * COLORS,)),
+            dma((3 * COLORS,)), dma((4 * COLORS,)), dma, dma((2 * COLORS,)),
+            dma, dma((PARTS * COLORS,)), dma((CUTS * COLORS,)), dma,
             dma, dma((5,)), dma((5,)), dma, dma, dma, dma, dma,
         ],
         compiler_params=pltpu.CompilerParams(
             collective_id=0, has_side_effects=True, vmem_limit_bytes=63 * 1024 * 1024),
         name="scatter_sum",
-    )(g_mat, g_vec, learn_rate.reshape(1, 1))
+    )(g_mat, g_vec, learn_rate.reshape(1))
     return out, vec, scales
 
 
@@ -387,7 +427,8 @@
                   scales_sem, g_sem, p_sem, m_sem, v_sem, s_sem, r_sem, ds_sem, dr_sem):
     own = COLORS * PARTS
     rows = p.shape[1]
-    step = min(rows, ROWS)
+    part = rows // CUTS
+    step = min(part, ROWS)
     me = lax.axis_index(axis_name)
     deltas = [s * (1 - 2 * lax.rem(me // s, 2)) for s in STRIDES]
     partner = me + 1 - 2 * lax.rem(me, 2)
@@ -400,8 +441,8 @@
     def loads(color, q):
         i = color * PARTS + q
         return (pltpu.make_async_copy(grad.at[i], g_buf.at[color], g_sem.at[color]),
-                pltpu.make_async_copy(m.at[i], m_out.at[i], m_sem.at[i]),
-                pltpu.make_async_copy(v.at[i], v_out.at[i], v_sem.at[i]),
+                pltpu.make_async_copy(m.at[i], m_out.at[i], m_sem.at[color]),
+                pltpu.make_async_copy(v.at[i], v_out.at[i], v_sem.at[color]),
                 pltpu.make_async_copy(p.at[i], p_buf.at[color], p_sem.at[color]))
 
     def across(index):
@@ -415,12 +456,13 @@
         flips = ((), (), (b2,), (), (b1,), (b2,), (b1, b2))[stage]
         return color, sum((deltas[f] for f in flips), me)
 
-    def push(stage, axis, q):
+    def push(stage, axis, q, span=None):
         color, owner = route(stage, axis)
         index = owner * own + color * PARTS + q
-        k = (stage * 3 + axis) * PARTS + q
-        return pltpu.make_async_remote_copy(
-            src_ref=out.at[index], dst_ref=out.at[index], send_sem=s_sem.at[k], recv_sem=r_sem.at[k],
+        place = 2 * q + stage if stage < 2 else stage * PARTS + q
+        ref = out.at[index] if span is None else out.at[index, span]
+        return pltpu.make_async_remote_copy(
+            src_ref=ref, dst_ref=ref, send_sem=s_sem, recv_sem=r_sem.at[axis * 14 + lax.rem(place, 14)],
             device_id=(peers[axis],), device_id_type=MESH_ID)
 
     def land(stage, axis, q):
@@ -428,10 +470,10 @@
         push(stage, axis, q).wait_recv()
         across((owner + deltas[axis]) * own + color * PARTS + q).start()
 
-    def update(color, q):
+    def update(color, q, first=0, count=None):
         i = color * PARTS + q
 
-        @pl.loop(0, rows // step)
+        @pl.loop(first // step, (first + (count or rows)) // step)
         def _(r):
             s = pl.ds(pl.multiple_of(r * step, step), step)
             new_m, new_v = adam_moments(g_buf[color, s, :] * scales[0:1, :], m_out[i, s, :], v_out[i, s, :])
@@ -453,10 +495,15 @@
         for color in range(COLORS):
             for copy in loads(color, q):
                 copy.wait()
-            update(color, q)
-            if q == 0 and color == 0:
-                pl.semaphore_wait(barrier, 4)
-            push(0, color, q).start()
+            if q == 0:
+                for i in range(CUTS):
+                    update(color, q, i * part, part)
+                    if color == 0 and i == 0:
+                        pl.semaphore_wait(barrier, 4)
+                    push(0, color, q, pl.ds(i * part, part)).start()
+            else:
+                update(color, q)
+                push(0, color, q).start()
             push(1, (color + 1) % 3, q).start()
             across(me * own + color * PARTS + q).start()
             if q + 1 < PARTS:
@@ -478,11 +525,10 @@
                 land(stage - 1, axis, q)
         each(PARTS, body)
 
-    for stage in range(7):
-        def body(q, stage=stage):
-            for axis in range(3):
-                push(stage, axis, q).wait_send()
-        each(PARTS, body)
+    sent = out.at[pl.ds(0, 7 * own)]
+    pltpu.make_async_remote_copy(
+        src_ref=sent, dst_ref=sent, send_sem=s_sem, recv_sem=r_sem.at[0],
+        device_id=(partner,), device_id_type=MESH_ID).wait_send()
     half = pltpu.make_async_remote_copy(
         src_ref=out.at[pl.ds(0, 8 * own)], dst_ref=out.at[pl.ds(0, 8 * own)], send_sem=ds_sem, recv_sem=dr_sem,
         device_id=(partner,), device_id_type=MESH_ID)
@@ -505,9 +551,9 @@
 
     def copies(i):
         part = pl.ds(i * span, span)
-        return (pltpu.make_async_copy(held.at[part], out.at[part], sem.at[0, i]),
-                pltpu.make_async_copy(m_held.at[i], m_out.at[i], sem.at[1, i]),
-                pltpu.make_async_copy(v_held.at[i], v_out.at[i], sem.at[2, i]))
+        return (pltpu.make_async_copy(held.at[part], out.at[part], sem.at[0, i % AHEAD]),
+                pltpu.make_async_copy(m_held.at[i], m_out.at[i], sem.at[1, i % AHEAD]),
+                pltpu.make_async_copy(v_held.at[i], v_out.at[i], sem.at[2, i % AHEAD]))
 
     scales_load = pltpu.make_async_copy(scales_in, scales, scales_sem)
     scales_load.start()
@@ -588,8 +634,8 @@
         out_specs=[vmem_spec] * 3,
         scratch_shapes=[
             pltpu.VMEM((COLORS, rows, 128), jnp.float32), pltpu.VMEM((COLORS, rows, 128), jnp.float32),
-            pltpu.VMEM((2, 128), jnp.float32), dma, dma((COLORS,)), dma((COLORS,)), dma((own,)), dma((own,)),
-            dma((7 * 3 * PARTS,)), dma((7 * 3 * PARTS,)), dma, dma],
+            pltpu.VMEM((2, 128), jnp.float32), dma, dma((COLORS,)), dma((COLORS,)), dma((COLORS,)), dma((COLORS,)),
+            dma, dma((3 * 14,)), dma, dma],
         compiler_params=pltpu.CompilerParams(
             collective_id=1, has_side_effects=True, vmem_limit_bytes=SMALL_VMEM),
         name="gather_update",
@@ -604,7 +650,7 @@
         scratch_shapes=[
             pltpu.VMEM((RING, rows, 128), jnp.float32), pltpu.VMEM((4, 1, n_vec), jnp.float32),
             pltpu.VMEM((2, 128), jnp.float32),
-            dma((RING,)), dma((RING,)), dma((3, own)), dma((4,)), dma((3,)), dma],
+            dma((RING,)), dma((RING,)), dma((3, AHEAD)), dma((4,)), dma((3,)), dma],
         compiler_params=pltpu.CompilerParams(vmem_limit_bytes=SMALL_VMEM),
         name="write_out",
     )(*(pltpu.with_memory_space_constraint(a, pltpu.VMEM) for a in (full, new_m, new_v)),

time: 523 us -> 520 us (level)
  no operation moved by 1% of the time
where the time goes in v5:
time: 520 us
  Pallas kernels  519 us (100%)
    pallas_call x1, Pallas kernels, scatter_sum(): pl.pallas_call(functools.partial(scatter_kernel, axis_name, piece), out_s...  330 us
    pallas_call x1, Pallas kernels, gather_update(): pl.pallas_call(functools.partial(gather_kernel, axis_name), out_shape=(pl...  164 us
    pallas_call x1, Pallas kernels, gather_update(): pl.pallas_call(write_kernel, out_shape=(jax.ShapeDtypeStruct(full.shape,...  24 us

profile of v5, /device:TPU:0, one launch (start us, length us, event | category | flops | bytes accessed | tf_op | source)
XLA Modules:
  0.0 520.0 jit_solution(5637641634274346511)
XLA Ops:
  1.3 330.5 %scatter_sum.1 = (f32[1,1572864]{1,0:T(1,128)}, bf16[1,12582912]{1,0:T(2,128)(2,1)}, f32[1,26624]{1,0:T(1,128)}, f32[2,128]{1,0:T(2,128)}) custom-call(bf16[1,25165824]{1,0:T(2,128)(2,1)} %g.1, bf16[1,26624]{1,0:T(2,128)(2,1)} %gv.1, f32[1]{0:T(128)} %bitcast.15.lr), custom_call_target="tpu_custom_call" | custom-call | tf_op jit(solution)/shard_map/scatter_sum/pallas_call | solution.py:376
  331.7 164.2 %gather_update.1 = (bf16[192,1024,128]{2,1,0:T(8,128)(2,1)S(1)}, f32[12,1024,128]{2,1,0:T(8,128)S(1)}, f32[12,1024,128]{2,1,0:T(8,128)S(1)}) custom-call(f32[12,1024,128]{2,1,0:T(8,128)} %bitcast.20, f32[12,1024,128]{2,1,0:T(8,128)} %bitcast.16, f32[12,1024,128]{2,1,0:T(8,128)} %bitcast.18, f32[12,1024,128]{2,1,0:T(8,128)} %bitcast.19, ...), custom_call_target="tpu_custom_call" | custom-call | tf_op jit(solution)/shard_map/gather_update/pallas_call | solution.py:628
  496.0 24.0 %write_out.1 = (bf16[192,1024,128]{2,1,0:T(8,128)(2,1)}, f32[12,1024,128]{2,1,0:T(8,128)}, f32[12,1024,128]{2,1,0:T(8,128)}, f32[12,1024,128]{2,1,0:T(8,128)}, f...) custom-call(bf16[192,1024,128]{2,1,0:T(8,128)(2,1)S(1)} %get-tuple-element.22.held, ...), custom_call_target="tpu_custom_call" | custom-call | tf_op jit(solution)/shard_map/write_out/pallas_call | solution.py:645

commit v6 on v5

--- a/solution.py
+++ b/solution.py
@@ -28,6 +28,8 @@
 SMALL_VMEM = 3400 * 1024
 RING = 5
 AHEAD = 2
+SWAPS = 8
+PLACES = 20
 CUTS = 4
 MEAN_SCALE = 1.0 / 16.0
 
@@ -68,22 +70,21 @@
         return pltpu.make_async_remote_copy(
             src_ref=cut(g, offset(color, t) + core_step * piece),
             dst_ref=cut(pg, (color * STEPS + t) * chunk),
-            send_sem=ds_sem.at[color * 4 + lax.rem(t, 4)],
-            recv_sem=dr_sem.at[color * 8 + lax.rem(t, 8)],
+            send_sem=ds_sem, recv_sem=dr_sem.at[color * SWAPS + lax.rem(t, SWAPS)],
             device_id=(partner,), device_id_type=MESH_ID)
 
     def swap_early(color, t):
         k = color * 2 + t
         return pltpu.make_async_remote_copy(
             src_ref=cut(g, offset(color, t) + core_step * piece), dst_ref=b_buf.at[k],
-            send_sem=ds_sem.at[color * 4 + t], recv_sem=dr_sem.at[color * 8 + t],
+            send_sem=ds_sem, recv_sem=dr_sem.at[color * SWAPS + t],
             device_id=(partner,), device_id_type=MESH_ID)
 
     def swap_cut(color, i):
         s = pl.ds(i * part, part)
         return pltpu.make_async_remote_copy(
             src_ref=e_buf.at[color, :, s], dst_ref=b_buf.at[color * 2, :, s],
-            send_sem=ds_sem.at[color * 4], recv_sem=dc_sem.at[color * CUTS + i],
+            send_sem=ds_sem, recv_sem=dc_sem.at[color * CUTS + i],
             device_id=(partner,), device_id_type=MESH_ID)
 
     def load_e(color):
@@ -161,7 +162,7 @@
         src = half(v_full, 1 - core) if k == 0 else half(v_mean, core) if k == 4 else v_acc.at[k]
         return pltpu.make_async_remote_copy(
             src_ref=src, dst_ref=half(v_mean, core) if k == 4 else v_get.at[k],
-            send_sem=vs_sem.at[k], recv_sem=vr_sem.at[k],
+            send_sem=vs_sem, recv_sem=vr_sem.at[k],
             device_id=((partner, *peers, partner)[k],), device_id_type=MESH_ID)
 
     def norm_push(k):
@@ -197,7 +198,6 @@
         load_b(color, t).start()
 
     def more_swap(color, t):
-        swap(color, t - 4).wait_send()
         swap(color, t).start()
 
     for color in range(COLORS):
@@ -357,10 +357,11 @@
     drain(4 * PARTS - 3, 4 * PARTS, lambda c, t: push1(c, t).wait_send())
     push(r2, r2, s2_sem, r2_sem.at[0], 0).wait_send()
     push(r3, r3, s3_sem, r3_sem.at[0], 0).wait_send()
-    drain(STEPS - 4, STEPS, lambda c, t: swap(c, t).wait_send())
+    pltpu.make_async_remote_copy(
+        src_ref=pg, dst_ref=pg, send_sem=ds_sem, recv_sem=dr_sem.at[0],
+        device_id=(partner,), device_id_type=MESH_ID).wait_send()
     pltpu.make_async_copy(out, out, o_sem).wait()
-    for k in range(5):
-        vec_push(k).wait_send()
+    push(v_get, v_get, vs_sem, vr_sem.at[0], 0).wait_send()
     rest.wait_send()
     vec_store.wait()
     scale_store.wait()
@@ -392,7 +393,7 @@
             pltpu.VMEM((1, n_vec), jnp.bfloat16),
             pltpu.VMEM((1, n_vec), jnp.float32),
             pltpu.VMEM((4, 1, n_vec // 2), jnp.float32),
-            pltpu.VMEM((4, 1, n_vec // 2), jnp.float32),
+            pltpu.VMEM((5, 1, n_vec // 2), jnp.float32),
             pltpu.VMEM((1, n_vec), jnp.float32),
             pltpu.VMEM((1, 128), jnp.float32),
             pltpu.VMEM((DEVICES, 1, 128), jnp.float32),
@@ -400,10 +401,10 @@
             pltpu.SMEM((1,), jnp.float32),
             pltpu.VMEM((2, 128), jnp.float32),
             dma((2 * COLORS,)), dma((2 * COLORS,)), dma((COLORS,)),
-            dma((4 * COLORS,)), dma((8 * COLORS,)), dma((CUTS * COLORS,)),
+            dma, dma((SWAPS * COLORS,)), dma((CUTS * COLORS,)),
             dma((3 * COLORS,)), dma((4 * COLORS,)), dma, dma((2 * COLORS,)),
             dma, dma((PARTS * COLORS,)), dma((CUTS * COLORS,)), dma,
-            dma, dma((5,)), dma((5,)), dma, dma, dma, dma, dma,
+            dma, dma, dma((5,)), dma, dma, dma, dma, dma,
         ],
         compiler_params=pltpu.CompilerParams(
             collective_id=0, has_side_effects=True, vmem_limit_bytes=63 * 1024 * 1024),
@@ -459,10 +460,10 @@
     def push(stage, axis, q, span=None):
         color, owner = route(stage, axis)
         index = owner * own + color * PARTS + q
-        place = 2 * q + stage if stage < 2 else stage * PARTS + q
+        place = (3 * q, 3 * q + 1, 3 * PARTS + q, 3 * q + 2)[stage] if stage < 4 else stage * PARTS + q
         ref = out.at[index] if span is None else out.at[index, span]
         return pltpu.make_async_remote_copy(
-            src_ref=ref, dst_ref=ref, send_sem=s_sem, recv_sem=r_sem.at[axis * 14 + lax.rem(place, 14)],
+            src_ref=ref, dst_ref=ref, send_sem=s_sem, recv_sem=r_sem.at[axis * PLACES + lax.rem(place, PLACES)],
             device_id=(peers[axis],), device_id_type=MESH_ID)
 
     def land(stage, axis, q):
@@ -487,42 +488,44 @@
 
     scales_load = pltpu.make_async_copy(scales_in, scales, scales_sem)
     scales_load.start()
-    for color in range(COLORS):
-        for copy in loads(color, 0):
+
+    def fetch(color, q):
+        for copy in loads(color, q):
             copy.start()
+
+    fetch(0, 0)
     scales_load.wait()
+    fetch(1, 0)
     for q in range(PARTS):
         for color in range(COLORS):
             for copy in loads(color, q):
                 copy.wait()
-            if q == 0:
-                for i in range(CUTS):
-                    update(color, q, i * part, part)
-                    if color == 0 and i == 0:
-                        pl.semaphore_wait(barrier, 4)
-                    push(0, color, q, pl.ds(i * part, part)).start()
-            else:
-                update(color, q)
-                push(0, color, q).start()
-            push(1, (color + 1) % 3, q).start()
+            if q == 0 and color == 0:
+                fetch(2, 0)
+            for i in range(CUTS if q == 0 else 1):
+                count = rows // CUTS if q == 0 else rows
+                update(color, q, i * count, count)
+                if q == 0 and color == 0 and i == 0:
+                    pl.semaphore_wait(barrier, 4)
+                for k, stage in enumerate((0, 1, 3)):
+                    push(stage, (color + k) % 3, q, pl.ds(i * count, count)).start()
             across(me * own + color * PARTS + q).start()
             if q + 1 < PARTS:
-                for copy in loads(color, q + 1):
-                    copy.start()
-        if q >= 2:
+                fetch(color, q + 1)
+
+    def own_stage(q):
+        for axis in range(3):
+            for stage in (0, 1, 3):
+                land(stage, axis, q)
+            push(2, (axis + 1) % 3, q).start()
+
+    each(PARTS, own_stage)
+    for stage, last in ((4, 2), (5, 4), (6, 5), (None, 6)):
+        def body(q, stage=stage, last=last):
             for axis in range(3):
-                land(0, axis, q - 2)
-                land(1, axis, q - 2)
-    for q in range(PARTS):
-        for axis in range(3):
-            push(2, axis, q).start()
-            land(q % 2, axis, 2 + q // 2)
-    for stage in range(3, 8):
-        def body(q, stage=stage):
-            for axis in range(3):
-                if stage < 7:
+                if stage:
                     push(stage, axis, q).start()
-                land(stage - 1, axis, q)
+                land(last, axis, q)
         each(PARTS, body)
 
     sent = out.at[pl.ds(0, 7 * own)]
@@ -635,7 +638,7 @@
         scratch_shapes=[
             pltpu.VMEM((COLORS, rows, 128), jnp.float32), pltpu.VMEM((COLORS, rows, 128), jnp.float32),
             pltpu.VMEM((2, 128), jnp.float32), dma, dma((COLORS,)), dma((COLORS,)), dma((COLORS,)), dma((COLORS,)),
-            dma, dma((3 * 14,)), dma, dma],
+            dma, dma((3 * PLACES,)), dma, dma],
         compiler_params=pltpu.CompilerParams(
             collective_id=1, has_side_effects=True, vmem_limit_bytes=SMALL_VMEM),
         name="gather_update",

time: 520 us -> 519 us (level)
  no operation moved by 1% of the time
where the time goes in v6:
time: 519 us
  Pallas kernels  518 us (100%)
    pallas_call x1, Pallas kernels, scatter_sum(): pl.pallas_call(functools.partial(scatter_kernel, axis_name, piece), out_s...  330 us
    pallas_call x1, Pallas kernels, gather_update(): pl.pallas_call(functools.partial(gather_kernel, axis_name), out_shape=(pl...  163 us
    pallas_call x1, Pallas kernels, gather_update(): pl.pallas_call(write_kernel, out_shape=(jax.ShapeDtypeStruct(full.shape,...  24 us

profile of v6, /device:TPU:0, one launch (start us, length us, event | category | flops | bytes accessed | tf_op | source)
XLA Modules:
  0.0 518.8 jit_solution(7758705629314129454)
XLA Ops:
  1.3 330.3 %scatter_sum.1 = (f32[1,1572864]{1,0:T(1,128)}, bf16[1,12582912]{1,0:T(2,128)(2,1)}, f32[1,26624]{1,0:T(1,128)}, f32[2,128]{1,0:T(2,128)}) custom-call(bf16[1,25165824]{1,0:T(2,128)(2,1)} %g.1, bf16[1,26624]{1,0:T(2,128)(2,1)} %gv.1, f32[1]{0:T(128)} %bitcast.15.lr), custom_call_target="tpu_custom_call" | custom-call | tf_op jit(solution)/shard_map/scatter_sum/pallas_call | solution.py:377
  331.6 163.2 %gather_update.1 = (bf16[192,1024,128]{2,1,0:T(8,128)(2,1)S(1)}, f32[12,1024,128]{2,1,0:T(8,128)S(1)}, f32[12,1024,128]{2,1,0:T(8,128)S(1)}) custom-call(f32[12,1024,128]{2,1,0:T(8,128)} %bitcast.20, f32[12,1024,128]{2,1,0:T(8,128)} %bitcast.16, f32[12,1024,128]{2,1,0:T(8,128)} %bitcast.18, f32[12,1024,128]{2,1,0:T(8,128)} %bitcast.19, ...), custom_call_target="tpu_custom_call" | custom-call | tf_op jit(solution)/shard_map/gather_update/pallas_call | solution.py:631
  494.8 24.0 %write_out.1 = (bf16[192,1024,128]{2,1,0:T(8,128)(2,1)}, f32[12,1024,128]{2,1,0:T(8,128)}, f32[12,1024,128]{2,1,0:T(8,128)}, f32[12,1024,128]{2,1,0:T(8,128)}, f...) custom-call(bf16[192,1024,128]{2,1,0:T(8,128)(2,1)S(1)} %get-tuple-element.22.held, ...), custom_call_target="tpu_custom_call" | custom-call | tf_op jit(solution)/shard_map/write_out/pallas_call | solution.py:648

commit v7 on v6

--- a/solution.py
+++ b/solution.py
@@ -25,8 +25,9 @@
 DEVICES = 16
 WIDTH = 4096
 ROWS = 64
-SMALL_VMEM = 3400 * 1024
-RING = 5
+SMALL_VMEM = 1344 * 1024
+RING = 3
+KEEP = 4
 AHEAD = 2
 SWAPS = 8
 PLACES = 20
@@ -424,12 +425,12 @@
     return p - rate * (direction + decay * p)
 
 
-def gather_kernel(axis_name, grad, p, m, v, scales_in, out, m_out, v_out, g_buf, p_buf, scales,
-                  scales_sem, g_sem, p_sem, m_sem, v_sem, s_sem, r_sem, ds_sem, dr_sem):
+def gather_kernel(axis_name, grad, p, m, v, scales_in, out, m_out, v_out, p_out, g_buf, p_buf, scales,
+                  scales_sem, load_sem, s_sem, r_sem, ds_sem, dr_sem):
     own = COLORS * PARTS
     rows = p.shape[1]
-    part = rows // CUTS
-    step = min(part, ROWS)
+    tile = rows // 2
+    step = min(tile // 2, ROWS)
     me = lax.axis_index(axis_name)
     deltas = [s * (1 - 2 * lax.rem(me // s, 2)) for s in STRIDES]
     partner = me + 1 - 2 * lax.rem(me, 2)
@@ -439,12 +440,16 @@
     for dev in (partner, *peers):
         pl.semaphore_signal(barrier, inc=1, device_id=(dev,), device_id_type=MESH_ID)
 
-    def loads(color, q):
+    def fetch(n):
+        q, color, h = n // (2 * COLORS), n // 2 % COLORS, n % 2
         i = color * PARTS + q
-        return (pltpu.make_async_copy(grad.at[i], g_buf.at[color], g_sem.at[color]),
-                pltpu.make_async_copy(m.at[i], m_out.at[i], m_sem.at[color]),
-                pltpu.make_async_copy(v.at[i], v_out.at[i], v_sem.at[color]),
-                pltpu.make_async_copy(p.at[i], p_buf.at[color], p_sem.at[color]))
+        s = pl.ds(h * tile, tile)
+        p_dst = p_out.at[i, s] if i < KEEP else p_buf.at[h]
+        for src, dst in ((grad, g_buf.at[h]), (m, m_out.at[i, s]), (v, v_out.at[i, s]), (p, p_dst)):
+            pltpu.make_async_copy(src.at[i, s], dst, load_sem.at[h]).start()
+
+    def arrived(n):
+        pltpu.make_async_copy(m.at[pl.ds(0, 2)], m_out.at[pl.ds(0, 2)], load_sem.at[n % 2]).wait()
 
     def across(index):
         return pltpu.make_async_remote_copy(
@@ -471,16 +476,20 @@
         push(stage, axis, q).wait_recv()
         across((owner + deltas[axis]) * own + color * PARTS + q).start()
 
-    def update(color, q, first=0, count=None):
+    def update(color, q, h, first, count):
         i = color * PARTS + q
 
-        @pl.loop(first // step, (first + (count or rows)) // step)
+        @pl.loop(first // step, (first + count) // step)
         def _(r):
-            s = pl.ds(pl.multiple_of(r * step, step), step)
-            new_m, new_v = adam_moments(g_buf[color, s, :] * scales[0:1, :], m_out[i, s, :], v_out[i, s, :])
+            t = pl.ds(pl.multiple_of(r * step, step), step)
+            s = pl.ds(pl.multiple_of(h * tile + r * step, step), step)
+            new_m, new_v = adam_moments(g_buf[h, t, :] * scales[0:1, :], m_out[i, s, :], v_out[i, s, :])
             m_out[i, s, :] = new_m
             v_out[i, s, :] = new_v
-            new_p = adam_param(p_buf[color, s, :], new_m, new_v, scales[1:2, :], WEIGHT_DECAY)
+            old_p = p_out[i, s, :] if i < KEEP else p_buf[h, t, :]
+            new_p = adam_param(old_p, new_m, new_v, scales[1:2, :], WEIGHT_DECAY)
+            if i < KEEP:
+                p_out[i, s, :] = new_p
             out[me * own + i, s, :] = new_p.astype(jnp.bfloat16)
 
     def each(count, body):
@@ -488,30 +497,24 @@
 
     scales_load = pltpu.make_async_copy(scales_in, scales, scales_sem)
     scales_load.start()
-
-    def fetch(color, q):
-        for copy in loads(color, q):
-            copy.start()
-
-    fetch(0, 0)
+    fetch(0)
     scales_load.wait()
-    fetch(1, 0)
-    for q in range(PARTS):
-        for color in range(COLORS):
-            for copy in loads(color, q):
-                copy.wait()
-            if q == 0 and color == 0:
-                fetch(2, 0)
-            for i in range(CUTS if q == 0 else 1):
-                count = rows // CUTS if q == 0 else rows
-                update(color, q, i * count, count)
-                if q == 0 and color == 0 and i == 0:
-                    pl.semaphore_wait(barrier, 4)
-                for k, stage in enumerate((0, 1, 3)):
-                    push(stage, (color + k) % 3, q, pl.ds(i * count, count)).start()
+    fetch(1)
+    for n in range(2 * own):
+        q, color, h = n // (2 * COLORS), n // 2 % COLORS, n % 2
+        cuts = 2 if n < 2 else 1
+        arrived(n)
+        for c in range(cuts):
+            count = tile // cuts
+            update(color, q, h, c * count, count)
+            if n == 0 and c == 0:
+                pl.semaphore_wait(barrier, 4)
+            for k, stage in enumerate((0, 1, 3)):
+                push(stage, (color + k) % 3, q, pl.ds(h * tile + c * count, count)).start()
+        if h:
             across(me * own + color * PARTS + q).start()
-            if q + 1 < PARTS:
-                fetch(color, q + 1)
+        if n + 2 < 2 * own:
+            fetch(n + 2)
 
     def own_stage(q):
         for axis in range(3):
@@ -539,24 +542,31 @@
     half.wait_send()
 
 
-def write_kernel(held, m_held, v_held, p, scales_in, g_vec, p_vec, m_vec, v_vec,
+def write_kernel(held, m_held, v_held, p_held, p, scales_in, g_vec, p_vec, m_vec, v_vec,
                  out, p_out, m_out, v_out, pv_out, mv_out, vv_out,
                  p_buf, vec_buf, scales, in_sem, out_sem, sem, vec_sem, vec_out_sem, scales_sem):
     own, rows, _ = p.shape
     step = min(rows, ROWS)
     span = held.shape[0] // own
 
-    def load(i):
-        return pltpu.make_async_copy(p.at[i], p_buf.at[i % RING], in_sem.at[i % RING])
-
-    def store(i):
-        return pltpu.make_async_copy(p_buf.at[i % RING], p_out.at[i], out_sem.at[i % RING])
+    tile = rows // 2
+    tiles = 2 * (own - KEEP)
+
+    def place(n):
+        return KEEP + n // 2, pl.ds(n % 2 * tile, tile)
+
+    def load(n):
+        return pltpu.make_async_copy(p.at[place(n)], p_buf.at[n % RING], in_sem.at[n % RING])
+
+    def store(n):
+        return pltpu.make_async_copy(p_buf.at[n % RING], p_out.at[place(n)], out_sem.at[n % RING])
 
     def copies(i):
         part = pl.ds(i * span, span)
-        return (pltpu.make_async_copy(held.at[part], out.at[part], sem.at[0, i % AHEAD]),
-                pltpu.make_async_copy(m_held.at[i], m_out.at[i], sem.at[1, i % AHEAD]),
-                pltpu.make_async_copy(v_held.at[i], v_out.at[i], sem.at[2, i % AHEAD]))
+        pairs = [(held.at[part], out.at[part]), (m_held.at[i], m_out.at[i]), (v_held.at[i], v_out.at[i])]
+        if i < KEEP:
+            pairs.append((p_held.at[i], p_out.at[i]))
+        return [pltpu.make_async_copy(src, dst, sem.at[k, i % AHEAD]) for k, (src, dst) in enumerate(pairs)]
 
     scales_load = pltpu.make_async_copy(scales_in, scales, scales_sem)
     scales_load.start()
@@ -579,38 +589,39 @@
         for copy in vec_stores:
             copy.start()
 
-    for i in range(RING - 1):
-        load(i).start()
+    for n in range(RING - 1):
+        load(n).start()
     for copy in vec_loads:
         copy.start()
     for i in range(AHEAD):
         for copy in copies(i):
             copy.start()
     scales_load.wait()
-    for i in range(own):
-        load(i).wait()
-
-        @pl.loop(0, rows // step)
+    for n in range(tiles):
+        load(n).wait()
+        i = KEEP + n // 2
+
+        @pl.loop(0, tile // step)
         def _(r):
-            s = pl.ds(pl.multiple_of(r * step, step), step)
-            p_buf[i % RING, s, :] = adam_param(
-                p_buf[i % RING, s, :], m_held[i, s, :], v_held[i, s, :], scales[1:2, :], WEIGHT_DECAY)
-
-        store(i).start()
-        if i + RING - 1 < own:
-            if i:
-                store(i - 1).wait()
-            load(i + RING - 1).start()
-        if i + AHEAD < own:
-            for copy in copies(i):
+            t = pl.ds(pl.multiple_of(r * step, step), step)
+            s = pl.ds(pl.multiple_of(n % 2 * tile + r * step, step), step)
+            p_buf[n % RING, t, :] = adam_param(
+                p_buf[n % RING, t, :], m_held[i, s, :], v_held[i, s, :], scales[1:2, :], WEIGHT_DECAY)
+
+        store(n).start()
+        if n + RING - 1 < tiles:
+            if n:
+                store(n - 1).wait()
+            load(n + RING - 1).start()
+        for j in range(n * (own - AHEAD) // tiles, (n + 1) * (own - AHEAD) // tiles):
+            for copy in copies(j):
                 copy.wait()
-            for copy in copies(i + AHEAD):
+            for copy in copies(j + AHEAD):
                 copy.start()
-        if i == 0:
+        if n == 0:
             vec_update()
-
-    for i in range(own - RING, own):
-        store(i).wait()
+    for n in range(tiles - RING, tiles):
+        store(n).wait()
     for i in range(own - AHEAD, own):
         for copy in copies(i):
             copy.wait()
@@ -628,16 +639,17 @@
     vmem_spec = pl.BlockSpec(memory_space=pltpu.VMEM)
     grad, p, m, v = (a.reshape(own, rows, 128) for a in (grad, p, m, v))
     p_vec, m_vec, v_vec = (a.reshape(1, n_vec) for a in (p_vec, m_vec, v_vec))
-    full, new_m, new_v = pl.pallas_call(
+    full, new_m, new_v, new_p = pl.pallas_call(
         functools.partial(gather_kernel, axis_name),
         out_shape=(pltpu.VMEM((group_size * own, rows, 128), jnp.bfloat16),
                    pltpu.VMEM((own, rows, 128), jnp.float32),
-                   pltpu.VMEM((own, rows, 128), jnp.float32)),
+                   pltpu.VMEM((own, rows, 128), jnp.float32),
+                   pltpu.VMEM((KEEP, rows, 128), jnp.float32)),
         in_specs=[any_spec] * 5,
-        out_specs=[vmem_spec] * 3,
+        out_specs=[vmem_spec] * 4,
         scratch_shapes=[
-            pltpu.VMEM((COLORS, rows, 128), jnp.float32), pltpu.VMEM((COLORS, rows, 128), jnp.float32),
-            pltpu.VMEM((2, 128), jnp.float32), dma, dma((COLORS,)), dma((COLORS,)), dma((COLORS,)), dma((COLORS,)),
+            pltpu.VMEM((2, rows // 2, 128), jnp.float32), pltpu.VMEM((2, rows // 2, 128), jnp.float32),
+            pltpu.VMEM((2, 128), jnp.float32), dma, dma((2,)),
             dma, dma((3 * PLACES,)), dma, dma],
         compiler_params=pltpu.CompilerParams(
             collective_id=1, has_side_effects=True, vmem_limit_bytes=SMALL_VMEM),
@@ -648,15 +660,15 @@
     full, new_p, new_m, new_v, *vecs = pl.pallas_call(
         write_kernel,
         out_shape=(jax.ShapeDtypeStruct(full.shape, full.dtype), flat, flat, flat, line, line, line),
-        in_specs=[vmem_spec] * 3 + [any_spec] * 6,
+        in_specs=[vmem_spec] * 4 + [any_spec] * 6,
         out_specs=[any_spec] * 7,
         scratch_shapes=[
-            pltpu.VMEM((RING, rows, 128), jnp.float32), pltpu.VMEM((4, 1, n_vec), jnp.float32),
+            pltpu.VMEM((RING, rows // 2, 128), jnp.float32), pltpu.VMEM((4, 1, n_vec), jnp.float32),
             pltpu.VMEM((2, 128), jnp.float32),
-            dma((RING,)), dma((RING,)), dma((3, AHEAD)), dma((4,)), dma((3,)), dma],
+            dma((RING,)), dma((RING,)), dma((4, AHEAD)), dma((4,)), dma((3,)), dma],
         compiler_params=pltpu.CompilerParams(vmem_limit_bytes=SMALL_VMEM),
         name="write_out",
-    )(*(pltpu.with_memory_space_constraint(a, pltpu.VMEM) for a in (full, new_m, new_v)),
+    )(*(pltpu.with_memory_space_constraint(a, pltpu.VMEM) for a in (full, new_m, new_v, new_p)),
       p, scales, grad_vec, p_vec, m_vec, v_vec)
     return (*(a.reshape(piece) for a in (new_p, new_m, new_v)), *(a.reshape(n_vec) for a in vecs),
             full.reshape(group_size * piece))

time: 519 us -> 520 us (level)
  no operation moved by 1% of the time
where the time goes in v7:
time: 520 us
  Pallas kernels  518 us (100%)
    pallas_call x1, Pallas kernels, scatter_sum(): pl.pallas_call(functools.partial(scatter_kernel, axis_name, piece), out_s...  330 us
    pallas_call x1, Pallas kernels, gather_update(): pl.pallas_call(functools.partial(gather_kernel, axis_name), out_shape=(pl...  163 us
    pallas_call x1, Pallas kernels, gather_update(): pl.pallas_call(write_kernel, out_shape=(jax.ShapeDtypeStruct(full.shape,...  25.3 us

profile of v7, /device:TPU:0, one launch (start us, length us, event | category | flops | bytes accessed | tf_op | source)
XLA Modules:
  0.0 519.7 jit_solution(5438154874072182067)
XLA Ops:
  1.3 330.3 %scatter_sum.1 = (f32[1,1572864]{1,0:T(1,128)}, bf16[1,12582912]{1,0:T(2,128)(2,1)}, f32[1,26624]{1,0:T(1,128)}, f32[2,128]{1,0:T(2,128)}) custom-call(bf16[1,25165824]{1,0:T(2,128)(2,1)} %g.1, bf16[1,26624]{1,0:T(2,128)(2,1)} %gv.1, f32[1]{0:T(128)} %bitcast.15.lr), custom_call_target="tpu_custom_call" | custom-call | tf_op jit(solution)/shard_map/scatter_sum/pallas_call | solution.py:378
  331.6 162.7 %gather_update.1 = (bf16[192,1024,128]{2,1,0:T(8,128)(2,1)S(1)}, f32[12,1024,128]{2,1,0:T(8,128)S(1)}, f32[12,1024,128]{2,1,0:T(8,128)S(1)}, f32[4,1024,128]{2,1,0:T(8,128)S(1)}) custom-call(f32[12,1024,128]{2,1,0:T(8,128)} %bitcast.20, f32[12,1024,128]{2,1,0:T(8,128)} %bitcast.16, f32[12,1024,128]{2,1,0:T(8,128)} %bitcast.18, f32[12,1024,128]{2,1,0:T(8,128)} %bitcast.19, ...), custom_call_target="tpu_custom_call" | custom-call | tf_op jit(solution)/shard_map/gather_update/pallas_call | solution.py:642
  494.4 25.3 %write_out.1 = (bf16[192,1024,128]{2,1,0:T(8,128)(2,1)}, f32[12,1024,128]{2,1,0:T(8,128)}, f32[12,1024,128]{2,1,0:T(8,128)}, f32[12,1024,128]{2,1,0:T(8,128)}, f...) custom-call(bf16[192,1024,128]{2,1,0:T(8,128)(2,1)S(1)} %get-tuple-element.23.held, ...), custom_call_target="tpu_custom_call" | custom-call | tf_op jit(solution)/shard_map/write_out/pallas_call | solution.py:660

commit v8 on v7

--- a/solution.py
+++ b/solution.py
@@ -25,10 +25,10 @@
 DEVICES = 16
 WIDTH = 4096
 ROWS = 64
-SMALL_VMEM = 1344 * 1024
-RING = 3
+SMALL_VMEM = 1792 * 1024
+RING = 5
 KEEP = 4
-AHEAD = 2
+AHEAD = 3
 SWAPS = 8
 PLACES = 20
 CUTS = 4

time: 520 us -> 520 us (level)
  no operation moved by 1% of the time
where the time goes in v8:
time: 520 us; the launch traced here: 519 us
  Pallas kernels  518 us (100%)
    pallas_call x1, Pallas kernels, scatter_sum(): pl.pallas_call(functools.partial(scatter_kernel, axis_name, piece), out_s...  330 us
    pallas_call x1, Pallas kernels, gather_update(): pl.pallas_call(functools.partial(gather_kernel, axis_name), out_shape=(pl...  163 us
    pallas_call x1, Pallas kernels, gather_update(): pl.pallas_call(write_kernel, out_shape=(jax.ShapeDtypeStruct(full.shape,...  24.6 us

profile of v8, /device:TPU:0, one launch (start us, length us, event | category | flops | bytes accessed | tf_op | source)
XLA Modules:
  0.0 519.0 jit_solution(11137153956558590564)
XLA Ops:
  1.3 330.3 %scatter_sum.1 = (f32[1,1572864]{1,0:T(1,128)}, bf16[1,12582912]{1,0:T(2,128)(2,1)}, f32[1,26624]{1,0:T(1,128)}, f32[2,128]{1,0:T(2,128)}) custom-call(bf16[1,25165824]{1,0:T(2,128)(2,1)} %g.1, bf16[1,26624]{1,0:T(2,128)(2,1)} %gv.1, f32[1]{0:T(128)} %bitcast.15.lr), custom_call_target="tpu_custom_call" | custom-call | tf_op jit(solution)/shard_map/scatter_sum/pallas_call | solution.py:378
  331.6 162.7 %gather_update.1 = (bf16[192,1024,128]{2,1,0:T(8,128)(2,1)S(1)}, f32[12,1024,128]{2,1,0:T(8,128)S(1)}, f32[12,1024,128]{2,1,0:T(8,128)S(1)}, f32[4,1024,128]{2,1,0:T(8,128)S(1)}) custom-call(f32[12,1024,128]{2,1,0:T(8,128)} %bitcast.20, f32[12,1024,128]{2,1,0:T(8,128)} %bitcast.16, f32[12,1024,128]{2,1,0:T(8,128)} %bitcast.18, f32[12,1024,128]{2,1,0:T(8,128)} %bitcast.19, ...), custom_call_target="tpu_custom_call" | custom-call | tf_op jit(solution)/shard_map/gather_update/pallas_call | solution.py:642
  494.4 24.6 %write_out.1 = (bf16[192,1024,128]{2,1,0:T(8,128)(2,1)}, f32[12,1024,128]{2,1,0:T(8,128)}, f32[12,1024,128]{2,1,0:T(8,128)}, f32[12,1024,128]{2,1,0:T(8,128)}, f...) custom-call(bf16[192,1024,128]{2,1,0:T(8,128)(2,1)S(1)} %get-tuple-element.23.held, ...), custom_call_target="tpu_custom_call" | custom-call | tf_op jit(solution)/shard_map/write_out/pallas_call | solution.py:660

commit v9 on v7

--- a/solution.py
+++ b/solution.py
@@ -25,9 +25,9 @@
 DEVICES = 16
 WIDTH = 4096
 ROWS = 64
-SMALL_VMEM = 1344 * 1024
+SMALL_VMEM = 2048 * 1024
 RING = 3
-KEEP = 4
+KEEP = 3
 AHEAD = 2
 SWAPS = 8
 PLACES = 20
@@ -549,17 +549,13 @@
     step = min(rows, ROWS)
     span = held.shape[0] // own
 
-    tile = rows // 2
-    tiles = 2 * (own - KEEP)
-
-    def place(n):
-        return KEEP + n // 2, pl.ds(n % 2 * tile, tile)
+    tiles = own - KEEP
 
     def load(n):
-        return pltpu.make_async_copy(p.at[place(n)], p_buf.at[n % RING], in_sem.at[n % RING])
+        return pltpu.make_async_copy(p.at[KEEP + n], p_buf.at[n % RING], in_sem.at[n % RING])
 
     def store(n):
-        return pltpu.make_async_copy(p_buf.at[n % RING], p_out.at[place(n)], out_sem.at[n % RING])
+        return pltpu.make_async_copy(p_buf.at[n % RING], p_out.at[KEEP + n], out_sem.at[n % RING])
 
     def copies(i):
         part = pl.ds(i * span, span)
@@ -599,14 +595,13 @@
     scales_load.wait()
     for n in range(tiles):
         load(n).wait()
-        i = KEEP + n // 2
-
-        @pl.loop(0, tile // step)
+        i = KEEP + n
+
+        @pl.loop(0, rows // step)
         def _(r):
-            t = pl.ds(pl.multiple_of(r * step, step), step)
-            s = pl.ds(pl.multiple_of(n % 2 * tile + r * step, step), step)
-            p_buf[n % RING, t, :] = adam_param(
-                p_buf[n % RING, t, :], m_held[i, s, :], v_held[i, s, :], scales[1:2, :], WEIGHT_DECAY)
+            s = pl.ds(pl.multiple_of(r * step, step), step)
+            p_buf[n % RING, s, :] = adam_param(
+                p_buf[n % RING, s, :], m_held[i, s, :], v_held[i, s, :], scales[1:2, :], WEIGHT_DECAY)
 
         store(n).start()
         if n + RING - 1 < tiles:
@@ -663,7 +658,7 @@
         in_specs=[vmem_spec] * 4 + [any_spec] * 6,
         out_specs=[any_spec] * 7,
         scratch_shapes=[
-            pltpu.VMEM((RING, rows // 2, 128), jnp.float32), pltpu.VMEM((4, 1, n_vec), jnp.float32),
+            pltpu.VMEM((RING, rows, 128), jnp.float32), pltpu.VMEM((4, 1, n_vec), jnp.float32),
             pltpu.VMEM((2, 128), jnp.float32),
             dma((RING,)), dma((RING,)), dma((4, AHEAD)), dma((4,)), dma((3,)), dma],
         compiler_params=pltpu.CompilerParams(vmem_limit_bytes=SMALL_VMEM),

time: 520 us -> 518 us (level)
  no operation moved by 1% of the time
where the time goes in v9:
time: 518 us
  Pallas kernels  516 us (100%)
    pallas_call x1, Pallas kernels, scatter_sum(): pl.pallas_call(functools.partial(scatter_kernel, axis_name, piece), out_s...  330 us
    pallas_call x1, Pallas kernels, gather_update(): pl.pallas_call(functools.partial(gather_kernel, axis_name), out_shape=(pl...  163 us
    pallas_call x1, Pallas kernels, gather_update(): pl.pallas_call(write_kernel, out_shape=(jax.ShapeDtypeStruct(full.shape,...  23.2 us

profile of v9, /device:TPU:0, one launch (start us, length us, event | category | flops | bytes accessed | tf_op | source)
XLA Modules:
  0.0 517.5 jit_solution(4463435788952281249)
XLA Ops:
  1.3 330.3 %scatter_sum.1 = (f32[1,1572864]{1,0:T(1,128)}, bf16[1,12582912]{1,0:T(2,128)(2,1)}, f32[1,26624]{1,0:T(1,128)}, f32[2,128]{1,0:T(2,128)}) custom-call(bf16[1,25165824]{1,0:T(2,128)(2,1)} %g.1, bf16[1,26624]{1,0:T(2,128)(2,1)} %gv.1, f32[1]{0:T(128)} %bitcast.15.lr), custom_call_target="tpu_custom_call" | custom-call | tf_op jit(solution)/shard_map/scatter_sum/pallas_call | solution.py:378
  331.6 162.7 %gather_update.1 = (bf16[192,1024,128]{2,1,0:T(8,128)(2,1)S(1)}, f32[12,1024,128]{2,1,0:T(8,128)S(1)}, f32[12,1024,128]{2,1,0:T(8,128)S(1)}, f32[3,1024,128]{2,1,0:T(8,128)S(1)}) custom-call(f32[12,1024,128]{2,1,0:T(8,128)} %bitcast.20, f32[12,1024,128]{2,1,0:T(8,128)} %bitcast.16, f32[12,1024,128]{2,1,0:T(8,128)} %bitcast.18, f32[12,1024,128]{2,1,0:T(8,128)} %bitcast.19, ...), custom_call_target="tpu_custom_call" | custom-call | tf_op jit(solution)/shard_map/gather_update/pallas_call | solution.py:637
  494.4 23.2 %write_out.1 = (bf16[192,1024,128]{2,1,0:T(8,128)(2,1)}, f32[12,1024,128]{2,1,0:T(8,128)}, f32[12,1024,128]{2,1,0:T(8,128)}, f32[12,1024,128]{2,1,0:T(8,128)}, f...) custom-call(bf16[192,1024,128]{2,1,0:T(8,128)(2,1)S(1)} %get-tuple-element.23.held, ...), custom_call_target="tpu_custom_call" | custom-call | tf_op jit(solution)/shard_map/write_out/pallas_call | solution.py:655

commit v10 on v9

--- a/solution.py
+++ b/solution.py
@@ -28,7 +28,7 @@
 SMALL_VMEM = 2048 * 1024
 RING = 3
 KEEP = 3
-AHEAD = 2
+AHEAD = 3
 SWAPS = 8
 PLACES = 20
 CUTS = 4
@@ -95,7 +95,7 @@
     def push_cut(color, i):
         k, j = color * 3, color * 4 * PARTS
         s = pl.ds(i * part, part)
-        return push(stage.at[k, :, s], r1.at[j, :, s], s1_sem.at[k], r1_sem.at[color * 4], color)
+        return push(stage.at[k, :, s], r1.at[j, :, s], s1_sem.at[k], r1_sem.at[color * 2], color)
 
     def load_a(color, t):
         k = color * 2 + lax.rem(t, 2)
@@ -113,7 +113,7 @@
     def push1(color, t):
         k = color * 3 + lax.rem(t, 3)
         j = color * 4 * PARTS + t
-        return push(stage.at[k], r1.at[j], s1_sem.at[k], r1_sem.at[color * 4 + t // PARTS], color)
+        return push(stage.at[k], r1.at[j], s1_sem.at[k], r1_sem.at[color * 2 + t // (2 * PARTS)], color)
 
     def push2(color, t):
         j = color * 2 * PARTS + t - 4 * PARTS
@@ -129,9 +129,9 @@
         return push(r1.at[color * 4 * PARTS + 3 * PARTS - 1, :, s], r3.at[color * PARTS + PARTS - 1, :, s],
                     s3_sem, rc_sem.at[color * CUTS + i], (color + 2) % 3)
 
-    def unit1(color, u):
-        span = r1.at[pl.ds((color * 4 + u) * PARTS, PARTS)]
-        return push(span, span, s2_sem, r1_sem.at[color * 4 + u], color)
+    def unit1(color, pair):
+        span = r1.at[pl.ds((color * 2 + pair) * 2 * PARTS, 2 * PARTS)]
+        return push(span, span, s2_sem, r1_sem.at[color * 2 + pair], color)
 
     def unit2(color, w):
         span = r2.at[pl.ds((color * 2 + w) * PARTS, PARTS)]
@@ -308,7 +308,8 @@
 
     for unit in range(4, 8):
         for color in range(COLORS):
-            unit1(color, unit - 4).wait_recv()
+            if unit in (4, 6):
+                unit1(color, (unit - 4) // 2).wait_recv()
             if unit >= 6:
                 unit2(color, unit - 6).wait_recv()
         lo = unit * PARTS
@@ -403,7 +404,7 @@
             pltpu.VMEM((2, 128), jnp.float32),
             dma((2 * COLORS,)), dma((2 * COLORS,)), dma((COLORS,)),
             dma, dma((SWAPS * COLORS,)), dma((CUTS * COLORS,)),
-            dma((3 * COLORS,)), dma((4 * COLORS,)), dma, dma((2 * COLORS,)),
+            dma((3 * COLORS,)), dma((2 * COLORS,)), dma, dma((2 * COLORS,)),
             dma, dma((PARTS * COLORS,)), dma((CUTS * COLORS,)), dma,
             dma, dma, dma((5,)), dma, dma, dma, dma, dma,
         ],
@@ -557,12 +558,26 @@
     def store(n):
         return pltpu.make_async_copy(p_buf.at[n % RING], p_out.at[KEEP + n], out_sem.at[n % RING])
 
-    def copies(i):
-        part = pl.ds(i * span, span)
-        pairs = [(held.at[part], out.at[part]), (m_held.at[i], m_out.at[i]), (v_held.at[i], v_out.at[i])]
+    def spread(start, count, i):
+        part = pl.ds(start, count)
+        return pltpu.make_async_copy(held.at[part], out.at[part], sem.at[0, i % AHEAD])
+
+    def small(i):
+        pairs = [(m_held.at[i], m_out.at[i]), (v_held.at[i], v_out.at[i])]
         if i < KEEP:
             pairs.append((p_held.at[i], p_out.at[i]))
-        return [pltpu.make_async_copy(src, dst, sem.at[k, i % AHEAD]) for k, (src, dst) in enumerate(pairs)]
+        return [pltpu.make_async_copy(src, dst, sem.at[k + 1, i % AHEAD]) for k, (src, dst) in enumerate(pairs)]
+
+    def begin(i):
+        for c in range(4):
+            spread(i * span + c * (span // 4), span // 4, i).start()
+        for copy in small(i):
+            copy.start()
+
+    def end(i):
+        spread(i * span, span, i).wait()
+        for copy in small(i):
+            copy.wait()
 
     scales_load = pltpu.make_async_copy(scales_in, scales, scales_sem)
     scales_load.start()
@@ -590,8 +605,7 @@
     for copy in vec_loads:
         copy.start()
     for i in range(AHEAD):
-        for copy in copies(i):
-            copy.start()
+        begin(i)
     scales_load.wait()
     for n in range(tiles):
         load(n).wait()
@@ -609,17 +623,14 @@
                 store(n - 1).wait()
             load(n + RING - 1).start()
         for j in range(n * (own - AHEAD) // tiles, (n + 1) * (own - AHEAD) // tiles):
-            for copy in copies(j):
-                copy.wait()
-            for copy in copies(j + AHEAD):
-                copy.start()
+            end(j)
+            begin(j + AHEAD)
         if n == 0:
             vec_update()
     for n in range(tiles - RING, tiles):
         store(n).wait()
     for i in range(own - AHEAD, own):
-        for copy in copies(i):
-            copy.wait()
+        end(i)
     for copy in vec_stores:
         copy.wait()
 

time: 518 us -> 518 us (level)
  no operation moved by 1% of the time
where the time goes in v10:
time: 518 us
  Pallas kernels  516 us (100%)
    pallas_call x1, Pallas kernels, scatter_sum(): pl.pallas_call(functools.partial(scatter_kernel, axis_name, piece), out_s...  330 us
    pallas_call x1, Pallas kernels, gather_update(): pl.pallas_call(functools.partial(gather_kernel, axis_name), out_shape=(pl...  163 us
    pallas_call x1, Pallas kernels, gather_update(): pl.pallas_call(write_kernel, out_shape=(jax.ShapeDtypeStruct(full.shape,...  23.2 us

profile of v10, /device:TPU:0, one launch (start us, length us, event | category | flops | bytes accessed | tf_op | source)
XLA Modules:
  0.0 517.5 jit_solution(6579486948137168540)
XLA Ops:
  1.3 330.3 %scatter_sum.1 = (f32[1,1572864]{1,0:T(1,128)}, bf16[1,12582912]{1,0:T(2,128)(2,1)}, f32[1,26624]{1,0:T(1,128)}, f32[2,128]{1,0:T(2,128)}) custom-call(bf16[1,25165824]{1,0:T(2,128)(2,1)} %g.1, bf16[1,26624]{1,0:T(2,128)(2,1)} %gv.1, f32[1]{0:T(128)} %bitcast.15.lr), custom_call_target="tpu_custom_call" | custom-call | tf_op jit(solution)/shard_map/scatter_sum/pallas_call | solution.py:379
  331.6 162.7 %gather_update.1 = (bf16[192,1024,128]{2,1,0:T(8,128)(2,1)S(1)}, f32[12,1024,128]{2,1,0:T(8,128)S(1)}, f32[12,1024,128]{2,1,0:T(8,128)S(1)}, f32[3,1024,128]{2,1,0:T(8,128)S(1)}) custom-call(f32[12,1024,128]{2,1,0:T(8,128)} %bitcast.20, f32[12,1024,128]{2,1,0:T(8,128)} %bitcast.16, f32[12,1024,128]{2,1,0:T(8,128)} %bitcast.18, f32[12,1024,128]{2,1,0:T(8,128)} %bitcast.19, ...), custom_call_target="tpu_custom_call" | custom-call | tf_op jit(solution)/shard_map/gather_update/pallas_call | solution.py:648
  494.3 23.2 %write_out.1 = (bf16[192,1024,128]{2,1,0:T(8,128)(2,1)}, f32[12,1024,128]{2,1,0:T(8,128)}, f32[12,1024,128]{2,1,0:T(8,128)}, f32[12,1024,128]{2,1,0:T(8,128)}, f...) custom-call(bf16[192,1024,128]{2,1,0:T(8,128)(2,1)S(1)} %get-tuple-element.23.held, ...), custom_call_target="tpu_custom_call" | custom-call | tf_op jit(solution)/shard_map/write_out/pallas_call | solution.py:666

commit v11 on v10

--- a/solution.py
+++ b/solution.py
@@ -427,7 +427,7 @@
 
 
 def gather_kernel(axis_name, grad, p, m, v, scales_in, out, m_out, v_out, p_out, g_buf, p_buf, scales,
-                  scales_sem, load_sem, s_sem, r_sem, ds_sem, dr_sem):
+                  scales_sem, load_sem, s_sem, r_sem, t_sem, ds_sem, dr_sem):
     own = COLORS * PARTS
     rows = p.shape[1]
     tile = rows // 2
@@ -452,9 +452,10 @@
     def arrived(n):
         pltpu.make_async_copy(m.at[pl.ds(0, 2)], m_out.at[pl.ds(0, 2)], load_sem.at[n % 2]).wait()
 
-    def across(index):
+    def across(index, span=None):
+        ref = out.at[index] if span is None else out.at[index, span]
         return pltpu.make_async_remote_copy(
-            src_ref=out.at[index], dst_ref=out.at[index], send_sem=ds_sem, recv_sem=dr_sem,
+            src_ref=ref, dst_ref=ref, send_sem=ds_sem, recv_sem=dr_sem,
             device_id=(partner,), device_id_type=MESH_ID)
 
     def route(stage, axis):
@@ -471,6 +472,16 @@
         return pltpu.make_async_remote_copy(
             src_ref=ref, dst_ref=ref, send_sem=s_sem, recv_sem=r_sem.at[axis * PLACES + lax.rem(place, PLACES)],
             device_id=(peers[axis],), device_id_type=MESH_ID)
+
+    def tail(axis, c):
+        color, owner = route(6, axis)
+        index = color * PARTS + PARTS - 1
+        span = pl.ds(c * (rows // CUTS), rows // CUTS)
+        ref = out.at[owner * own + index, span]
+        copy = pltpu.make_async_remote_copy(
+            src_ref=ref, dst_ref=ref, send_sem=s_sem, recv_sem=t_sem.at[axis * CUTS + c],
+            device_id=(peers[axis],), device_id_type=MESH_ID)
+        return copy, across((owner + deltas[axis]) * own + index, span)
 
     def land(stage, axis, q):
         color, owner = route(stage, axis)
@@ -524,13 +535,26 @@
             push(2, (axis + 1) % 3, q).start()
 
     each(PARTS, own_stage)
-    for stage, last in ((4, 2), (5, 4), (6, 5), (None, 6)):
+    for stage, last, count in ((4, 2, PARTS), (5, 4, PARTS), (6, 5, PARTS - 1)):
         def body(q, stage=stage, last=last):
             for axis in range(3):
-                if stage:
-                    push(stage, axis, q).start()
+                push(stage, axis, q).start()
                 land(last, axis, q)
-        each(PARTS, body)
+        each(count, body)
+    tails = [tail(axis, c) for c in range(CUTS) for axis in range(3)]
+    for copy, _ in tails:
+        copy.start()
+    for axis in range(3):
+        land(5, axis, PARTS - 1)
+
+    def last_stage(q):
+        for axis in range(3):
+            land(6, axis, q)
+
+    each(PARTS - 1, last_stage)
+    for copy, onward in tails:
+        copy.wait_recv()
+        onward.start()
 
     sent = out.at[pl.ds(0, 7 * own)]
     pltpu.make_async_remote_copy(
@@ -656,7 +680,7 @@
         scratch_shapes=[
             pltpu.VMEM((2, rows // 2, 128), jnp.float32), pltpu.VMEM((2, rows // 2, 128), jnp.float32),
             pltpu.VMEM((2, 128), jnp.float32), dma, dma((2,)),
-            dma, dma((3 * PLACES,)), dma, dma],
+            dma, dma((3 * PLACES,)), dma((3 * CUTS,)), dma, dma],
         compiler_params=pltpu.CompilerParams(
             collective_id=1, has_side_effects=True, vmem_limit_bytes=SMALL_VMEM),
         name="gather_update",

time: 518 us -> 518 us (level)
  no operation moved by 1% of the time
where the time goes in v11:
time: 518 us; the launch traced here: 517 us
  Pallas kernels  516 us (100%)
    pallas_call x1, Pallas kernels, scatter_sum(): pl.pallas_call(functools.partial(scatter_kernel, axis_name, piece), out_s...  330 us
    pallas_call x1, Pallas kernels, gather_update(): pl.pallas_call(functools.partial(gather_kernel, axis_name), out_shape=(pl...  162 us
    pallas_call x1, Pallas kernels, gather_update(): pl.pallas_call(write_kernel, out_shape=(jax.ShapeDtypeStruct(full.shape,...  23.2 us

profile of v11, /device:TPU:0, one launch (start us, length us, event | category | flops | bytes accessed | tf_op | source)
XLA Modules:
  0.0 517.2 jit_solution(16926923217768226858)
XLA Ops:
  1.3 330.3 %scatter_sum.1 = (f32[1,1572864]{1,0:T(1,128)}, bf16[1,12582912]{1,0:T(2,128)(2,1)}, f32[1,26624]{1,0:T(1,128)}, f32[2,128]{1,0:T(2,128)}) custom-call(bf16[1,25165824]{1,0:T(2,128)(2,1)} %g.1, bf16[1,26624]{1,0:T(2,128)(2,1)} %gv.1, f32[1]{0:T(128)} %bitcast.15.lr), custom_call_target="tpu_custom_call" | custom-call | tf_op jit(solution)/shard_map/scatter_sum/pallas_call | solution.py:379
  331.6 162.4 %gather_update.1 = (bf16[192,1024,128]{2,1,0:T(8,128)(2,1)S(1)}, f32[12,1024,128]{2,1,0:T(8,128)S(1)}, f32[12,1024,128]{2,1,0:T(8,128)S(1)}, f32[3,1024,128]{2,1,0:T(8,128)S(1)}) custom-call(f32[12,1024,128]{2,1,0:T(8,128)} %bitcast.20, f32[12,1024,128]{2,1,0:T(8,128)} %bitcast.16, f32[12,1024,128]{2,1,0:T(8,128)} %bitcast.18, f32[12,1024,128]{2,1,0:T(8,128)} %bitcast.19, ...), custom_call_target="tpu_custom_call" | custom-call | tf_op jit(solution)/shard_map/gather_update/pallas_call | solution.py:672
  493.9 23.2 %write_out.1 = (bf16[192,1024,128]{2,1,0:T(8,128)(2,1)}, f32[12,1024,128]{2,1,0:T(8,128)}, f32[12,1024,128]{2,1,0:T(8,128)}, f32[12,1024,128]{2,1,0:T(8,128)}, f...) custom-call(bf16[192,1024,128]{2,1,0:T(8,128)(2,1)S(1)} %get-tuple-element.23.held, ...), custom_call_target="tpu_custom_call" | custom-call | tf_op jit(solution)/shard_map/write_out/pallas_call | solution.py:690
